TPU v7x, 128 devices: a whole 4x4x4 slice. The times are simulated.
128 devices in a mesh: gx: 2 (over core), gy: 4 (over x), gz: 16 (over z, y).
Axes of the slice: x: 4, y: 4, z: 4, core: 2. Of those that a mesh axis runs over, the one named last changes fastest.
Arguments:
- right_side: float32 [96, 192, 768], P('gx', 'gy', 'gz'), may hold values from -6 to 6
- face_coef: float32 [3, 96, 192, 768], P(None, 'gx', 'gy', 'gz'), may hold values from 0.3 to 3
- absorption: float32 [96, 192, 768], P('gx', 'gy', 'gz'), may hold values from 0.001 to 0.01
Outputs:
- solution: float32 [96, 192, 768], P('gx', 'gy', 'gz')
- residual: float32 [96, 192, 768], P('gx', 'gy', 'gz')
- relative_norm: float32 [], replicated
All inputs are finite; a program needn't handle non-finite values.
Results may differ from a plain program's by a relative error of at most 0.0003.
Values sent between devices are 32-bit elements.
No kernel may reach another device: no remote copies, remote signals or barrier semaphores. Data moves between devices by JAX's collectives and lax.ppermute only.
A program may use at most 192 MiB of HBM per device.

v0:
```python
import jax
import jax.numpy as jnp
from jax import lax
from jax.sharding import Mesh
from jax.sharding import PartitionSpec as P

LEVELS = 5
SWEEPS = 3
BOTTOM = 6
GX_GY_GZ = ("gx", "gy", "gz_0", "gz_1")
GZ = ("gz_0", "gz_1")


cheb_low = 0.25
cheb_high = 2.0


def with_halo(value, sides, width, wrap):
    edges = {}
    for axis, dim in sides:
        devices, length = lax.axis_size(axis), value.shape[dim]
        up = [(i, (i + 1) % devices) for i in range(devices if wrap else devices - 1)]
        last = lax.slice_in_dim(value, length - width, length, axis=dim)
        leading = lax.slice_in_dim(value, 0, width, axis=dim)
        edges[dim] = lax.ppermute(last, axis, up), lax.ppermute(
            leading, axis, [(b, a) for a, b in up]
        )
    done = []
    for _, dim in sides:
        low, high = edges[dim]
        around = [(width, width) if d in done else (0, 0) for d in range(value.ndim)]
        value = jnp.concatenate([jnp.pad(low, around), value, jnp.pad(high, around)], axis=dim)
        done.append(dim)
    return value


def from_behind(value, axis, by):
    devices = lax.axis_size(axis)
    pairs = [(i, i + by) for i in range(devices) if 0 <= i + by < devices]
    return lax.ppermute(value, axis, pairs)


def over_axes(value, axes):
    for axis in axes:
        value = lax.psum(value, axis)
    return value


def apply_stencil(field, stencil, weight, padded):
    low_x = padded[:-2, 1:-1, 1:-1]
    high_x = padded[2:, 1:-1, 1:-1]
    low_y = padded[1:-1, :-2, 1:-1]
    high_y = padded[1:-1, 2:, 1:-1]
    low_z = padded[1:-1, 1:-1, :-2]
    high_z = padded[1:-1, 1:-1, 2:]
    flux = stencil[0] * (field - low_x) + stencil[3] * (field - high_x)
    flux = flux + stencil[1] * (field - low_y) + stencil[4] * (field - high_y)
    flux = flux + stencil[2] * (field - low_z) + stencil[5] * (field - high_z)
    return stencil[6] * field + weight * flux


def inverse_diagonal(stencil, weight):
    total = stencil[0] + stencil[3] + stencil[1] + stencil[4] + stencil[2] + stencil[5]
    return 1.0 / (stencil[6] + weight * total)


def chebyshev(iterate, source, stencil, weight, sweeps, from_zero, pad_field):
    centre = 0.5 * (cheb_high + cheb_low)
    half_width = 0.5 * (cheb_high - cheb_low)
    cheb_ratio = centre / half_width
    cheb_rho = 1.0 / cheb_ratio
    scaling = inverse_diagonal(stencil, weight)
    if from_zero:
        remainder = source
    else:
        remainder = source - apply_stencil(iterate, stencil, weight, pad_field(iterate))
    update = scaling * remainder * (1.0 / centre)
    for sweep in range(sweeps):
        iterate = iterate + update
        if sweep + 1 < sweeps:
            remainder = source - apply_stencil(iterate, stencil, weight, pad_field(iterate))
            next_rho = 1.0 / (2.0 * cheb_ratio - cheb_rho)
            update = next_rho * cheb_rho * update + 2.0 * next_rho / half_width * (
                scaling * remainder
            )
            cheb_rho = next_rho
    return iterate


def conjugate(source, stencil, weight, pad_field, total):
    iterate = jnp.zeros_like(source)
    remainder = source
    search = source
    norm_now = total(remainder * remainder)
    for step in range(BOTTOM):
        applied = apply_stencil(search, stencil, weight, pad_field(search))
        step_size = norm_now / total(search * applied)
        iterate = iterate + step_size * search
        if step + 1 < BOTTOM:
            remainder = remainder - step_size * applied
            norm_next = total(remainder * remainder)
            search = remainder + norm_next / norm_now * search
            norm_now = norm_next
    return iterate


def average_cells(field):
    blocks = field.reshape(field.shape[0] // 2, 2, field.shape[1] // 2, 2, field.shape[2] // 2, 2)
    return jnp.sum(blocks, axis=(1, 3, 5)) * 0.125


def average_faces(faces):
    halves = (faces.shape[1] // 2, 2, faces.shape[2] // 2, 2, faces.shape[3] // 2, 2)
    along_x = faces[0].reshape(halves)[:, 0]
    along_y = faces[1].reshape(halves)[:, :, :, 0]
    along_z = faces[2].reshape(halves)[..., 0]
    return (
        jnp.stack(
            [
                jnp.sum(along_x, axis=(2, 4)),
                jnp.sum(along_y, axis=(1, 4)),
                jnp.sum(along_z, axis=(1, 3)),
            ]
        )
        * 0.25
    )


def repeat_cells(field):
    shape = field.shape
    wide = jnp.broadcast_to(
        field[:, None, :, None, :, None], (shape[0], 2, shape[1], 2, shape[2], 2)
    )
    return wide.reshape(2 * shape[0], 2 * shape[1], 2 * shape[2])


def pad_zero(field):
    return jnp.pad(field, 1)


def halo_field(field):
    return with_halo(field, (("gx", 0), ("gy", 1), (GZ, 2)), 1, False)


def prepare(faces, cells):
    above_x = from_behind(faces[0, :1], "gx", -1)
    above_y = from_behind(faces[1, :, :1], "gy", -1)
    above_z = from_behind(faces[2, :, :, :1], GZ, -1)
    high_x = jnp.concatenate([faces[0, 1:], above_x], axis=0)
    high_y = jnp.concatenate([faces[1, :, 1:], above_y], axis=1)
    high_z = jnp.concatenate([faces[2, :, :, 1:], above_z], axis=2)
    return jnp.stack([faces[0], faces[1], faces[2], high_x, high_y, high_z, cells])


def assemble(flat, count, block):
    count_x = lax.axis_size("gx")
    count_y = lax.axis_size("gy")
    count_z = lax.axis_size(GZ)
    grid = flat.reshape(count_x, count_y, count_z, count, block[0], block[1], block[2])
    grid = jnp.transpose(grid, (3, 0, 4, 1, 5, 2, 6))
    return grid.reshape(count, count_x * block[0], count_y * block[1], count_z * block[2])


def shards(right_side, face_coef, absorption):
    source_sq = over_axes(jnp.sum(right_side * right_side), GX_GY_GZ)
    stencils = []
    faces = face_coef
    cells = absorption
    for level in range(LEVELS):
        stencils.append(prepare(faces, cells))
        if level + 1 < LEVELS:
            faces = average_faces(faces)
            cells = average_cells(cells)
    sources = []
    iterates = []
    source = right_side
    for level in range(LEVELS - 1):
        weight = 0.25**level
        iterate = chebyshev(
            jnp.zeros_like(source), source, stencils[level], weight, SWEEPS, True, halo_field
        )
        remainder = source - apply_stencil(iterate, stencils[level], weight, halo_field(iterate))
        sources.append(source)
        iterates.append(iterate)
        source = average_cells(remainder)
    coarse = stencils[LEVELS - 1]
    block = source.shape
    weight_low = 0.25 ** (LEVELS - 1)
    flat_coef = lax.all_gather(coarse.reshape(-1), GX_GY_GZ, axis=0, tiled=True)
    flat_source = lax.all_gather(source.reshape(-1), GX_GY_GZ, axis=0, tiled=True)
    whole_coef = assemble(flat_coef, 7, block)
    whole_source = assemble(flat_source, 1, block)[0]
    whole = conjugate(whole_source, whole_coef, weight_low, pad_zero, jnp.sum)
    starts = (
        lax.axis_index("gx") * block[0],
        lax.axis_index("gy") * block[1],
        lax.axis_index(GZ) * block[2],
    )
    correction = lax.dynamic_slice(whole, starts, block)
    for level in reversed(range(LEVELS - 1)):
        weight = 0.25**level
        iterate = iterates[level] + repeat_cells(correction)
        correction = chebyshev(
            iterate, sources[level], stencils[level], weight, SWEEPS, False, halo_field
        )
    residual = right_side - apply_stencil(correction, stencils[0], 1.0, halo_field(correction))
    residual_sq = over_axes(jnp.sum(residual * residual), GX_GY_GZ)
    relative_norm = jnp.sqrt(residual_sq / source_sq)
    return (correction, residual, relative_norm)


def solution(mesh):
    torus = Mesh(
        mesh.devices.reshape(mesh.shape["gx"], mesh.shape["gy"], 4, 4), ("gx", "gy", "gz_0", "gz_1")
    )
    in_specs = (P("gx", "gy", GZ), P(None, "gx", "gy", GZ), P("gx", "gy", GZ))
    out_specs = (P("gx", "gy", GZ), P("gx", "gy", GZ), P())
    return jax.shard_map(
        shards, mesh=torus, in_specs=in_specs, out_specs=out_specs, check_vma=False
    )
```

profile of v0, /device:TPU:8, one launch (start us, length us, event | category | flops | bytes accessed | tf_op | source)
XLA Modules:
  0.0 1233.5 jit_solution(8616450484737864457)
XLA Ops:
  25.2 15.4 %reshape_squeeze.37 = f32[24,2,24,2,24,2]{5,4,3,2,1,0:T(8,128)} reshape(f32[1,48,48,48]{3,2,1,0:T(8,128)} %get-tuple-element.74) | data formatting | bytes 884736 | tf_op jit(solution)/shard_map/reshape;squeeze | solution.py:115
  40.6 7.8 slice_reduce_fusion.1
  48.4 15.4 %reshape_squeeze.38 = f32[24,2,24,2,24,2]{5,4,3,2,1,0:T(8,128)} reshape(f32[1,48,48,48]{3,2,1,0:T(8,128)} %get-tuple-element.73) | data formatting | bytes 884736 | tf_op jit(solution)/shard_map/reshape;squeeze | solution.py:116
  63.8 11.8 slice_reduce_fusion
  75.6 15.4 %reshape_squeeze.36 = f32[24,2,24,2,24,2]{5,4,3,2,1,0:T(8,128)} reshape(f32[1,48,48,48]{3,2,1,0:T(8,128)} %get-tuple-element.72) | data formatting | bytes 884736 | tf_op jit(solution)/shard_map/reshape;squeeze | solution.py:114
  91.0 7.0 slice_reduce_fusion.2
  153.9 5.8 multiply_multiply_fusion
  174.5 5.1 collective-permute-start.5
  192.0 11.1 multiply_add_fusion.1
  217.9 4.9 collective-permute-start.11
  237.0 9.9 fusion.122
  261.8 5.1 collective-permute-start.20
  276.0 15.4 %reshape.86 = f32[24,2,24,2,24,2]{5,4,3,2,1,0:T(8,128)} reshape(f32[48,48,48]{2,1,0:T(8,128)} %param.5) | data formatting | bytes 884736 | tf_op jit(solution)/shard_map/reshape | solution.py:108
  297.1 10.8 reduce_sum.306
  321.5 10.6 fusion.97
  332.1 15.4 %reshape.87 = f32[24,2,24,2,24,2]{5,4,3,2,1,0:T(8,128)} reshape(f32[48,48,48]{2,1,0:T(8,128)} %fusion.97) | data formatting | bytes 884736 | tf_op jit(solution)/shard_map/reshape | solution.py:108
  347.5 10.8 reduce_sum.310
  361.3 5.3 collective-permute-start.26
  366.6 5.1 collective-permute-start.28
  379.4 5.7 collective-permute-done.29
  390.9 6.2 collective-permute-start.34
  460.1 6.1 collective-permute-start.47
  491.5 5.4 collective-permute-start.55
  515.0 5.7 collective-permute-start.64
  553.7 5.8 collective-permute-start.70
  561.4 4.9 collective-permute-start.68
  575.4 5.8 collective-permute-start.76
  594.3 5.8 collective-permute-start.82
  622.0 76.1 %all-reduce.106 = f32[3456]{0:T(1024)} all-reduce(f32[3456]{0:T(1024)} %dynamic-update-slice), channel_id=1, replica_groups=mesh['gx'=2,'gy'=4,'gz_0'=4,'gz_1'=4] {'gx','gy','gz_0','gz_1'}, use_global_device_ids=true, to_apply=%add.106 | all-reduce | flops 3456 | bytes 27648
  709.8 4.9 reshape.93
  714.7 5.6 fusion.769
  872.8 6.0 collective-permute-start.115
  892.2 6.0 collective-permute-start.121
  919.7 5.9 collective-permute-start.127
  933.2 5.3 collective-permute-done.128
  943.7 6.0 collective-permute-start.133
  981.5 9.7 broadcast_in_dim.11
  991.1 17.3 %reshape.97 = f32[48,48,48]{2,1,0:T(8,128)} reshape(f32[24,2,24,2,24,2]{5,4,3,2,1,0:T(8,128)} %broadcast_in_dim.11) | data formatting | bytes 884736 | tf_op jit(solution)/shard_map/reshape | solution.py:134
  1040.2 10.7 multiply_add_fusion
  1055.7 5.4 collective-permute-start.151
  1066.7 5.2 collective-permute-start.149
  1084.1 10.8 fusion.744
  1109.8 4.9 collective-permute-start.155
  1126.6 9.9 fusion.30
  1168.5 12.2 multiply_reduce_fusion.1
  1185.2 11.8 all-reduce.110
  1197.0 14.6 %all-reduce.109 = (f32[]{:T(128)}, f32[]{:T(128)}) all-reduce(f32[]{:T(128)} %get-tuple-element.7, f32[]{:T(128)} %get-tuple-element.8), channel_id=1, replica_groups=mesh['gx'=2,'gy'=4,'gz_0'=4,'gz_1'=4] {'gz_0'}, use_global_device_ids=true, to_apply=%region_35.36 | all-reduce | flops 2 | bytes 16 | tf_op jit(solution)/shard_map/psum | solution.py:45
  1211.7 12.2 all-reduce.108
  (771 shorter events, 718.8 us)
Async XLA Ops:
  7.2 702.7 %all-reduce.114.cloned.1.call-start = ((), (), s32[]{:S(2)}) async-start(), calls=%async_computation | async-start | bytes 196608
  8.5 145.3 %collective-permute-start = (f32[1,48,48]{2,1,0:T(8,128)}, f32[1,48,48]{2,1,0:T(8,128)}, u32[]{:S(2)}, u32[]{:S(2)}) collective-permute-start(f32[1,48,48]{2,1,0:T(8,128)} %slice_bitcast_fusion.13), channel_id=1, source_target_pairs={{64,0},{65,1},{66,2},{67,3},{68,4},{69,5},{70,6},{71,7},{72,8},{73... | collective-permute-start | bytes 27656 | tf_op jit(solution)/shard_map/ppermute | solution.py:40
  11.4 142.5 %collective-permute-start.1 = (f32[48,1,48]{2,1,0:T(1,128)}, f32[48,1,48]{2,1,0:T(1,128)}, u32[]{:S(2)}, u32[]{:S(2)}) collective-permute-start(f32[48,1,48]{2,1,0:T(1,128)} %slice_bitcast_fusion.12), channel_id=1, source_target_pairs={{16,0},{32,16},{48,32},{17,1},{33,17},{49,33},{18,2},{34,18},{50,3... | collective-permute-start | bytes 27656 | tf_op jit(solution)/shard_map/ppermute | solution.py:40
  17.5 134.2 %collective-permute-start.2 = (f32[48,48,1]{1,0,2:T(8,128)}, f32[48,48,1]{1,0,2:T(8,128)}, u32[]{:S(2)}, u32[]{:S(2)}) collective-permute-start(f32[48,48,1]{1,0,2:T(8,128)} %bitcast.326), channel_id=1, source_target_pairs={{1,0},{2,1},{3,2},{4,3},{5,4},{6,5},{7,6},{8,7},{9,8},{10,9},{11,1... | collective-permute-start | bytes 27656 | tf_op jit(solution)/shard_map/ppermute | solution.py:40
  164.4 19.4 %collective-permute-start.7 = (f32[48,48,1]{1,0,2:T(8,128)}, f32[48,48,1]{1,0,2:T(8,128)}, u32[]{:S(2)}, u32[]{:S(2)}) collective-permute-start(f32[48,48,1]{1,0,2:T(8,128)} %copy.152), channel_id=1, source_target_pairs={{0,1},{1,2},{2,3},{3,4},{4,5},{5,6},{6,7},{7,8},{8,9},{9,10},{10,1... | collective-permute-start | bytes 27656 | tf_op jit(solution)/shard_map/ppermute | solution.py:25
  171.7 16.6 %collective-permute-start.8 = (f32[48,48,1]{1,0,2:T(8,128)}, f32[48,48,1]{1,0,2:T(8,128)}, u32[]{:S(2)}, u32[]{:S(2)}) collective-permute-start(f32[48,48,1]{1,0,2:T(8,128)} %copy.154), channel_id=1, source_target_pairs={{1,0},{2,1},{3,2},{4,3},{5,4},{6,5},{7,6},{8,7},{9,8},{10,9},{11,1... | collective-permute-start | bytes 27656 | tf_op jit(solution)/shard_map/ppermute | solution.py:25
  174.5 16.0 %collective-permute-start.5 = (f32[48,1,48]{2,1,0:T(1,128)}, f32[48,1,48]{2,1,0:T(1,128)}, u32[]{:S(2)}, u32[]{:S(2)}) collective-permute-start(f32[48,1,48]{2,1,0:T(1,128)} %get-tuple-element.114), channel_id=1, source_target_pairs={{0,16},{16,32},{32,48},{1,17},{17,33},{33,49},{2,18},{18,34},{34,5... | collective-permute-start | bytes 27656 | tf_op jit(solution)/shard_map/ppermute | solution.py:25
  207.8 17.6 %collective-permute-start.13 = (f32[48,48,1]{1,0,2:T(8,128)}, f32[48,48,1]{1,0,2:T(8,128)}, u32[]{:S(2)}, u32[]{:S(2)}) collective-permute-start(f32[48,48,1]{1,0,2:T(8,128)} %copy.156), channel_id=1, source_target_pairs={{0,1},{1,2},{2,3},{3,4},{4,5},{5,6},{6,7},{7,8},{8,9},{9,10},{10,1... | collective-permute-start | bytes 27656 | tf_op jit(solution)/shard_map/ppermute | solution.py:25
  214.6 18.7 %collective-permute-start.14 = (f32[48,48,1]{1,0,2:T(8,128)}, f32[48,48,1]{1,0,2:T(8,128)}, u32[]{:S(2)}, u32[]{:S(2)}) collective-permute-start(f32[48,48,1]{1,0,2:T(8,128)} %copy.158), channel_id=1, source_target_pairs={{1,0},{2,1},{3,2},{4,3},{5,4},{6,5},{7,6},{8,7},{9,8},{10,9},{11,1... | collective-permute-start | bytes 27656 | tf_op jit(solution)/shard_map/ppermute | solution.py:25
  217.9 17.5 %collective-permute-start.11 = (f32[48,1,48]{2,1,0:T(1,128)}, f32[48,1,48]{2,1,0:T(1,128)}, u32[]{:S(2)}, u32[]{:S(2)}) collective-permute-start(f32[48,1,48]{2,1,0:T(1,128)} %get-tuple-element.110), channel_id=1, source_target_pairs={{0,16},{16,32},{32,48},{1,17},{17,33},{33,49},{2,18},{18,34},{34,5... | collective-permute-start | bytes 27656 | tf_op jit(solution)/shard_map/ppermute | solution.py:25
  251.7 18.4 %collective-permute-start.22 = (f32[48,48,1]{1,0,2:T(8,128)}, f32[48,48,1]{1,0,2:T(8,128)}, u32[]{:S(2)}, u32[]{:S(2)}) collective-permute-start(f32[48,48,1]{1,0,2:T(8,128)} %copy.162), channel_id=1, source_target_pairs={{0,1},{1,2},{2,3},{3,4},{4,5},{5,6},{6,7},{7,8},{8,9},{9,10},{10,1... | collective-permute-start | bytes 27656 | tf_op jit(solution)/shard_map/ppermute | solution.py:25
  259.1 52.8 %collective-permute-start.23 = (f32[48,48,1]{1,0,2:T(8,128)}, f32[48,48,1]{1,0,2:T(8,128)}, u32[]{:S(2)}, u32[]{:S(2)}) collective-permute-start(f32[48,48,1]{1,0,2:T(8,128)} %copy.164), channel_id=1, source_target_pairs={{1,0},{2,1},{3,2},{4,3},{5,4},{6,5},{7,6},{8,7},{9,8},{10,9},{11,1... | collective-permute-start | bytes 27656 | tf_op jit(solution)/shard_map/ppermute | solution.py:25
  261.8 53.6 %collective-permute-start.20 = (f32[48,1,48]{2,1,0:T(1,128)}, f32[48,1,48]{2,1,0:T(1,128)}, u32[]{:S(2)}, u32[]{:S(2)}) collective-permute-start(f32[48,1,48]{2,1,0:T(1,128)} %get-tuple-element.104), channel_id=1, source_target_pairs={{0,16},{16,32},{32,48},{1,17},{17,33},{33,49},{2,18},{18,34},{34,5... | collective-permute-start | bytes 27656 | tf_op jit(solution)/shard_map/ppermute | solution.py:25
  266.9 50.5 %collective-permute-start.21 = (f32[48,1,48]{2,1,0:T(1,128)}, f32[48,1,48]{2,1,0:T(1,128)}, u32[]{:S(2)}, u32[]{:S(2)}) collective-permute-start(f32[48,1,48]{2,1,0:T(1,128)} %get-tuple-element.105), channel_id=1, source_target_pairs={{16,0},{32,16},{48,32},{17,1},{33,17},{49,33},{18,2},{34,18},{50,3... | collective-permute-start | bytes 27656 | tf_op jit(solution)/shard_map/ppermute | solution.py:25
  268.2 51.3 %collective-permute-start.18 = (f32[1,48,48]{2,1,0:T(8,128)}, f32[1,48,48]{2,1,0:T(8,128)}, u32[]{:S(2)}, u32[]{:S(2)}) collective-permute-start(f32[1,48,48]{2,1,0:T(8,128)} %get-tuple-element.102), channel_id=1, source_target_pairs={{0,64},{1,65},{2,66},{3,67},{4,68},{5,69},{6,70},{7,71},{8,72},{9,... | collective-permute-start | bytes 27656 | tf_op jit(solution)/shard_map/ppermute | solution.py:25
  270.1 51.4 %collective-permute-start.19 = (f32[1,48,48]{2,1,0:T(8,128)}, f32[1,48,48]{2,1,0:T(8,128)}, u32[]{:S(2)}, u32[]{:S(2)}) collective-permute-start(f32[1,48,48]{2,1,0:T(8,128)} %get-tuple-element.103), channel_id=1, source_target_pairs={{64,0},{65,1},{66,2},{67,3},{68,4},{69,5},{70,6},{71,7},{72,8},{73... | collective-permute-start | bytes 27656 | tf_op jit(solution)/shard_map/ppermute | solution.py:25
  311.9 63.0 %collective-permute-start.84 = (f32[1,3,3]{2,0,1:T(1,128)}, f32[1,3,3]{2,0,1:T(1,128)S(1)}, u32[]{:S(2)}, u32[]{:S(2)}) collective-permute-start(f32[1,3,3]{2,0,1:T(1,128)} %squeeze.183), channel_id=1, source_target_pairs={{64,0},{65,1},{66,2},{67,3},{68,4},{69,5},{70,6},{71,7},{72,8},{73... | collective-permute-start | bytes 116 | tf_op jit(solution)/shard_map/ppermute | solution.py:40
  315.4 42.9 %collective-permute-start.15 = (f32[1,24,24]{2,1,0:T(8,128)}, f32[1,24,24]{2,1,0:T(8,128)S(1)}, u32[]{:S(2)}, u32[]{:S(2)}) collective-permute-start(f32[1,24,24]{2,1,0:T(8,128)} %slice_bitcast_fusion.16), channel_id=1, source_target_pairs={{64,0},{65,1},{66,2},{67,3},{68,4},{69,5},{70,6},{71,7},{72,8},{73... | collective-permute-start | bytes 6920 | tf_op jit(solution)/shard_map/ppermute | solution.py:40
  317.5 40.9 %collective-permute-start.16 = (f32[24,1,24]{2,1,0:T(1,128)}, f32[24,1,24]{2,1,0:T(1,128)}, u32[]{:S(2)}, u32[]{:S(2)}) collective-permute-start(f32[24,1,24]{2,1,0:T(1,128)} %slice_bitcast_fusion.15), channel_id=1, source_target_pairs={{16,0},{32,16},{48,32},{17,1},{33,17},{49,33},{18,2},{34,18},{50,3... | collective-permute-start | bytes 6920 | tf_op jit(solution)/shard_map/ppermute | solution.py:40
  319.5 38.8 %collective-permute-start.17 = (f32[24,24,1]{2,1,0:T(8,128)}, f32[24,24,1]{2,1,0:T(8,128)}, u32[]{:S(2)}, u32[]{:S(2)}) collective-permute-start(f32[24,24,1]{2,1,0:T(8,128)} %slice_bitcast_fusion.3), channel_id=1, source_target_pairs={{1,0},{2,1},{3,2},{4,3},{5,4},{6,5},{7,6},{8,7},{9,8},{10,9},{11,1... | collective-permute-start | bytes 6920 | tf_op jit(solution)/shard_map/ppermute | solution.py:40
  361.3 16.7 %collective-permute-start.26 = (f32[24,1,24]{2,1,0:T(1,128)S(1)}, f32[24,1,24]{2,1,0:T(1,128)S(1)}, u32[]{:S(2)}, u32[]{:S(2)}) collective-permute-start(f32[24,1,24]{2,1,0:T(1,128)S(1)} %get-tuple-element.157), channel_id=1, source_target_pairs={{0,16},{16,32},{32,48},{1,17},{17,33},{33,49},{2,18},{18,34},{34,5... | collective-permute-start | bytes 6920 | tf_op jit(solution)/shard_map/ppermute | solution.py:25
  404.7 19.4 %collective-permute-start.86 = (f32[3,3,1]{1,2,0:T(1,128)S(1)}, f32[3,3,1]{1,2,0:T(1,128)S(1)}, u32[]{:S(2)}, u32[]{:S(2)}) collective-permute-start(f32[3,3,1]{1,2,0:T(1,128)S(1)} %copy-done.72), channel_id=1, source_target_pairs={{1,0},{2,1},{3,2},{4,3},{5,4},{6,5},{7,6},{8,7},{9,8},{10,9},{11,1... | collective-permute-start | bytes 116 | tf_op jit(solution)/shard_map/ppermute | solution.py:40
  406.6 18.8 %collective-permute-start.38 = (f32[12,12,1]{1,2,0:T(1,128)S(1)}, f32[12,12,1]{1,2,0:T(1,128)S(1)}, u32[]{:S(2)}, u32[]{:S(2)}) collective-permute-start(f32[12,12,1]{1,2,0:T(1,128)S(1)} %copy-done.68), channel_id=1, source_target_pairs={{1,0},{2,1},{3,2},{4,3},{5,4},{6,5},{7,6},{8,7},{9,8},{10,9},{11,1... | collective-permute-start | bytes 1736 | tf_op jit(solution)/shard_map/ppermute | solution.py:40
  412.2 16.2 %collective-permute-start.41 = (f32[24,1,24]{2,1,0:T(1,128)S(1)}, f32[24,1,24]{2,1,0:T(1,128)}, u32[]{:S(2)}, u32[]{:S(2)}) collective-permute-start(f32[24,1,24]{2,1,0:T(1,128)S(1)} %get-tuple-element.147), channel_id=1, source_target_pairs={{0,16},{16,32},{32,48},{1,17},{17,33},{33,49},{2,18},{18,34},{34,5... | collective-permute-start | bytes 6920 | tf_op jit(solution)/shard_map/ppermute | solution.py:25
  417.3 24.9 %collective-permute-start.43 = (f32[24,24,1]{2,1,0:T(8,128)}, f32[24,24,1]{2,1,0:T(8,128)}, u32[]{:S(2)}, u32[]{:S(2)}) collective-permute-start(f32[24,24,1]{2,1,0:T(8,128)} %get-tuple-element.143), channel_id=1, source_target_pairs={{0,1},{1,2},{2,3},{3,4},{4,5},{5,6},{6,7},{7,8},{8,9},{9,10},{10,1... | collective-permute-start | bytes 6920 | tf_op jit(solution)/shard_map/ppermute | solution.py:25
  422.2 21.4 %collective-permute-start.44 = (f32[24,24,1]{2,1,0:T(8,128)}, f32[24,24,1]{2,1,0:T(8,128)}, u32[]{:S(2)}, u32[]{:S(2)}) collective-permute-start(f32[24,24,1]{2,1,0:T(8,128)} %get-tuple-element.144), channel_id=1, source_target_pairs={{1,0},{2,1},{3,2},{4,3},{5,4},{6,5},{7,6},{8,7},{9,8},{10,9},{11,1... | collective-permute-start | bytes 6920 | tf_op jit(solution)/shard_map/ppermute | solution.py:25
  424.1 16.2 %collective-permute-start.42 = (f32[24,1,24]{2,1,0:T(1,128)}, f32[24,1,24]{2,1,0:T(1,128)}, u32[]{:S(2)}, u32[]{:S(2)}) collective-permute-start(f32[24,1,24]{2,1,0:T(1,128)} %get-tuple-element.148), channel_id=1, source_target_pairs={{16,0},{32,16},{48,32},{17,1},{33,17},{49,33},{18,2},{34,18},{50,3... | collective-permute-start | bytes 6920 | tf_op jit(solution)/shard_map/ppermute | solution.py:25
  425.4 19.7 %collective-permute-start.39 = (f32[1,24,24]{2,1,0:T(8,128)}, f32[1,24,24]{2,1,0:T(8,128)}, u32[]{:S(2)}, u32[]{:S(2)}) collective-permute-start(f32[1,24,24]{2,1,0:T(8,128)} %get-tuple-element.145), channel_id=1, source_target_pairs={{0,64},{1,65},{2,66},{3,67},{4,68},{5,69},{6,70},{7,71},{8,72},{9,... | collective-permute-start | bytes 6920 | tf_op jit(solution)/shard_map/ppermute | solution.py:25
  428.5 16.6 %collective-permute-start.40 = (f32[1,24,24]{2,1,0:T(8,128)}, f32[1,24,24]{2,1,0:T(8,128)}, u32[]{:S(2)}, u32[]{:S(2)}) collective-permute-start(f32[1,24,24]{2,1,0:T(8,128)} %get-tuple-element.146), channel_id=1, source_target_pairs={{64,0},{65,1},{66,2},{67,3},{68,4},{69,5},{70,6},{71,7},{72,8},{73... | collective-permute-start | bytes 6920 | tf_op jit(solution)/shard_map/ppermute | solution.py:25
  440.3 34.3 %collective-permute-start.85 = (f32[3,1,3]{2,1,0:T(1,128)}, f32[3,1,3]{2,1,0:T(1,128)}, u32[]{:S(2)}, u32[]{:S(2)}) collective-permute-start(f32[3,1,3]{2,1,0:T(1,128)} %slice_bitcast_fusion.21), channel_id=1, source_target_pairs={{16,0},{32,16},{48,32},{17,1},{33,17},{49,33},{18,2},{34,18},{50,3... | collective-permute-start | bytes 116 | tf_op jit(solution)/shard_map/ppermute | solution.py:40
  460.1 18.4 %collective-permute-start.47 = (f32[12,1,12]{2,1,0:T(1,128)S(1)}, f32[12,1,12]{2,1,0:T(1,128)}, u32[]{:S(2)}, u32[]{:S(2)}) collective-permute-start(f32[12,1,12]{2,1,0:T(1,128)S(1)} %get-tuple-element.194), channel_id=1, source_target_pairs={{0,16},{16,32},{32,48},{1,17},{17,33},{33,49},{2,18},{18,34},{34,5... | collective-permute-start | bytes 1736 | tf_op jit(solution)/shard_map/ppermute | solution.py:25
  466.8 18.5 %collective-permute-start.49 = (f32[12,12,1]{2,1,0:T(8,128)}, f32[12,12,1]{2,1,0:T(8,128)}, u32[]{:S(2)}, u32[]{:S(2)}) collective-permute-start(f32[12,12,1]{2,1,0:T(8,128)} %get-tuple-element.192), channel_id=1, source_target_pairs={{0,1},{1,2},{2,3},{3,4},{4,5},{5,6},{6,7},{7,8},{8,9},{9,10},{10,1... | collective-permute-start | bytes 1736 | tf_op jit(solution)/shard_map/ppermute | solution.py:25
  483.3 16.9 %collective-permute-start.57 = (f32[1,6,6]{2,0,1:T(1,128)S(1)}, f32[1,6,6]{2,0,1:T(1,128)S(1)}, u32[]{:S(2)}, u32[]{:S(2)}) collective-permute-start(f32[1,6,6]{2,0,1:T(1,128)S(1)} %copy-done.70), channel_id=1, source_target_pairs={{64,0},{65,1},{66,2},{67,3},{68,4},{69,5},{70,6},{71,7},{72,8},{73... | collective-permute-start | bytes 440 | tf_op jit(solution)/shard_map/ppermute | solution.py:40
  487.2 16.0 %collective-permute-start.53 = (f32[12,1,12]{2,1,0:T(1,128)S(1)}, f32[12,1,12]{2,1,0:T(1,128)S(1)}, u32[]{:S(2)}, u32[]{:S(2)}) collective-permute-start(f32[12,1,12]{2,1,0:T(1,128)S(1)} %get-tuple-element.190), channel_id=1, source_target_pairs={{0,16},{16,32},{32,48},{1,17},{17,33},{33,49},{2,18},{18,34},{34,5... | collective-permute-start | bytes 1736 | tf_op jit(solution)/shard_map/ppermute | solution.py:25
  505.2 18.8 %collective-permute-start.59 = (f32[6,6,1]{1,2,0:T(1,128)}, f32[6,6,1]{1,2,0:T(1,128)S(1)}, u32[]{:S(2)}, u32[]{:S(2)}) collective-permute-start(f32[6,6,1]{1,2,0:T(1,128)} %squeeze.181), channel_id=1, source_target_pairs={{1,0},{2,1},{3,2},{4,3},{5,4},{6,5},{7,6},{8,7},{9,8},{10,9},{11,1... | collective-permute-start | bytes 440 | tf_op jit(solution)/shard_map/ppermute | solution.py:40
  509.5 17.5 %collective-permute-start.62 = (f32[12,1,12]{2,1,0:T(1,128)S(1)}, f32[12,1,12]{2,1,0:T(1,128)}, u32[]{:S(2)}, u32[]{:S(2)}) collective-permute-start(f32[12,1,12]{2,1,0:T(1,128)S(1)} %get-tuple-element.184), channel_id=1, source_target_pairs={{0,16},{16,32},{32,48},{1,17},{17,33},{33,49},{2,18},{18,34},{34,5... | collective-permute-start | bytes 1736 | tf_op jit(solution)/shard_map/ppermute | solution.py:25
  515.0 21.1 %collective-permute-start.64 = (f32[12,12,1]{2,1,0:T(8,128)}, f32[12,12,1]{2,1,0:T(8,128)}, u32[]{:S(2)}, u32[]{:S(2)}) collective-permute-start(f32[12,12,1]{2,1,0:T(8,128)} %get-tuple-element.180), channel_id=1, source_target_pairs={{0,1},{1,2},{2,3},{3,4},{4,5},{5,6},{6,7},{7,8},{8,9},{9,10},{10,1... | collective-permute-start | bytes 1736 | tf_op jit(solution)/shard_map/ppermute | solution.py:25
  553.7 18.3 %collective-permute-start.70 = (f32[6,6,1]{2,1,0:T(8,128)}, f32[6,6,1]{2,1,0:T(8,128)S(1)}, u32[]{:S(2)}, u32[]{:S(2)}) collective-permute-start(f32[6,6,1]{2,1,0:T(8,128)} %get-tuple-element.232), channel_id=1, source_target_pairs={{0,1},{1,2},{2,3},{3,4},{4,5},{5,6},{6,7},{7,8},{8,9},{9,10},{10,1... | collective-permute-start | bytes 440 | tf_op jit(solution)/shard_map/ppermute | solution.py:25
  575.4 17.7 %collective-permute-start.76 = (f32[6,6,1]{2,1,0:T(8,128)S(1)}, f32[6,6,1]{2,1,0:T(8,128)S(1)}, u32[]{:S(2)}, u32[]{:S(2)}) collective-permute-start(f32[6,6,1]{2,1,0:T(8,128)S(1)} %get-tuple-element.226), channel_id=1, source_target_pairs={{0,1},{1,2},{2,3},{3,4},{4,5},{5,6},{6,7},{7,8},{8,9},{9,10},{10,1... | collective-permute-start | bytes 440 | tf_op jit(solution)/shard_map/ppermute | solution.py:25
  594.3 18.0 %collective-permute-start.82 = (f32[6,6,1]{2,1,0:T(8,128)S(1)}, f32[6,6,1]{2,1,0:T(8,128)S(1)}, u32[]{:S(2)}, u32[]{:S(2)}) collective-permute-start(f32[6,6,1]{2,1,0:T(8,128)S(1)} %get-tuple-element.220), channel_id=1, source_target_pairs={{0,1},{1,2},{2,3},{3,4},{4,5},{5,6},{6,7},{7,8},{8,9},{9,10},{10,1... | collective-permute-start | bytes 440 | tf_op jit(solution)/shard_map/ppermute | solution.py:25
  811.5 15.9 %collective-permute-start.97 = (f32[6,6,1]{2,1,0:T(8,128)S(1)}, f32[6,6,1]{2,1,0:T(8,128)S(1)}, u32[]{:S(2)}, u32[]{:S(2)}) collective-permute-start(f32[6,6,1]{2,1,0:T(8,128)S(1)} %get-tuple-element.207), channel_id=1, source_target_pairs={{0,1},{1,2},{2,3},{3,4},{4,5},{5,6},{6,7},{7,8},{8,9},{9,10},{10,1... | collective-permute-start | bytes 440 | tf_op jit(solution)/shard_map/ppermute | solution.py:25
  828.7 16.0 %collective-permute-start.103 = (f32[6,6,1]{2,1,0:T(8,128)S(1)}, f32[6,6,1]{2,1,0:T(8,128)S(1)}, u32[]{:S(2)}, u32[]{:S(2)}) collective-permute-start(f32[6,6,1]{2,1,0:T(8,128)S(1)} %get-tuple-element.201), channel_id=1, source_target_pairs={{0,1},{1,2},{2,3},{3,4},{4,5},{5,6},{6,7},{7,8},{8,9},{9,10},{10,1... | collective-permute-start | bytes 440 | tf_op jit(solution)/shard_map/ppermute | solution.py:25
  1014.9 18.0 %collective-permute-start.145 = (f32[48,48,1]{1,0,2:T(8,128)}, f32[48,48,1]{1,0,2:T(8,128)}, u32[]{:S(2)}, u32[]{:S(2)}) collective-permute-start(f32[48,48,1]{1,0,2:T(8,128)} %copy.181), channel_id=1, source_target_pairs={{0,1},{1,2},{2,3},{3,4},{4,5},{5,6},{6,7},{7,8},{8,9},{9,10},{10,1... | collective-permute-start | bytes 27656 | tf_op jit(solution)/shard_map/ppermute | solution.py:25
  1055.7 21.1 %collective-permute-start.151 = (f32[48,48,1]{1,0,2:T(8,128)}, f32[48,48,1]{1,0,2:T(8,128)}, u32[]{:S(2)}, u32[]{:S(2)}) collective-permute-start(f32[48,48,1]{1,0,2:T(8,128)} %copy.185), channel_id=1, source_target_pairs={{0,1},{1,2},{2,3},{3,4},{4,5},{5,6},{6,7},{7,8},{8,9},{9,10},{10,1... | collective-permute-start | bytes 27656 | tf_op jit(solution)/shard_map/ppermute | solution.py:25
  1066.7 15.9 %collective-permute-start.149 = (f32[48,1,48]{2,1,0:T(1,128)}, f32[48,1,48]{2,1,0:T(1,128)}, u32[]{:S(2)}, u32[]{:S(2)}) collective-permute-start(f32[48,1,48]{2,1,0:T(1,128)} %get-tuple-element.90), channel_id=1, source_target_pairs={{0,16},{16,32},{32,48},{1,17},{17,33},{33,49},{2,18},{18,34},{34,5... | collective-permute-start | bytes 27656 | tf_op jit(solution)/shard_map/ppermute | solution.py:25
  1099.6 19.7 %collective-permute-start.157 = (f32[48,48,1]{1,0,2:T(8,128)}, f32[48,48,1]{1,0,2:T(8,128)}, u32[]{:S(2)}, u32[]{:S(2)}) collective-permute-start(f32[48,48,1]{1,0,2:T(8,128)} %copy.189), channel_id=1, source_target_pairs={{0,1},{1,2},{2,3},{3,4},{4,5},{5,6},{6,7},{7,8},{8,9},{9,10},{10,1... | collective-permute-start | bytes 27656 | tf_op jit(solution)/shard_map/ppermute | solution.py:25
  1141.3 19.7 %collective-permute-start.163 = (f32[48,48,1]{1,0,2:T(8,128)}, f32[48,48,1]{1,0,2:T(8,128)}, u32[]{:S(2)}, u32[]{:S(2)}) collective-permute-start(f32[48,48,1]{1,0,2:T(8,128)} %copy.193), channel_id=1, source_target_pairs={{0,1},{1,2},{2,3},{3,4},{4,5},{5,6},{6,7},{7,8},{8,9},{9,10},{10,1... | collective-permute-start | bytes 27656 | tf_op jit(solution)/shard_map/ppermute | solution.py:25
  1148.7 16.0 %collective-permute-start.164 = (f32[48,48,1]{1,0,2:T(8,128)}, f32[48,48,1]{1,0,2:T(8,128)}, u32[]{:S(2)}, u32[]{:S(2)}) collective-permute-start(f32[48,48,1]{1,0,2:T(8,128)} %copy.195), channel_id=1, source_target_pairs={{1,0},{2,1},{3,2},{4,3},{5,4},{6,5},{7,6},{8,7},{9,8},{10,9},{11,1... | collective-permute-start | bytes 27656 | tf_op jit(solution)/shard_map/ppermute | solution.py:25
  (191 other events, 2539.8 us)
Sparse Core Ops, SparseCore 0:
  553.8 155.9 all-reduce.113
where the time goes:
time: 1260 us; the launch traced here: 1230 us
  starting transfers between devices  433 us (34%)
  local copies, waits for them, and re-layouts  370 us (29%)
  other arithmetic  232 us (18%)
  blocking collectives  119 us (9%)
  waiting for transfers between devices  45.4 us (4%)
  between operations  35 us (3%)
    ppermute x75, starting transfers between devices, with_halo(): lax.ppermute(last, axis, up)  290 us
    ppermute x75, starting transfers between devices, with_halo(): lax.ppermute(leading, axis, [(b, a) for a, b in up])  120 us
    unnamed x1, blocking collectives  76.1 us
    add x20, other arithmetic, chebyshev(): iterate = iterate + update  70.6 us
    slice x82, local copies, waits for them, and re-layouts, with_halo(): last = lax.slice_in_dim(value, length - width, length, axis=dim)  52.4 us
    psum x4, blocking collectives, over_axes(): value = lax.psum(value, axis)  43.1 us
    ppermute x75, waiting for transfers between devices, with_halo(): lax.ppermute(leading, axis, [(b, a) for a, b in up])  39.9 us
    reshape x5, local copies, waits for them, and re-layouts, average_cells(): field.reshape(field.shape[0] // 2, 2, field.shape[1] // 2, 2, field.shape...  38.3 us
  transfers between devices with their start and end apart: 166, of which 26 were waited for; matrix products, arithmetic and copies ran while one was open for 29% of the time, Pallas kernels for 0%

commit v1 on v0

v1 whole, which is shorter than its diff:
```python
import functools

import jax
import jax.numpy as jnp
from jax import lax
from jax.experimental import pallas as pl
from jax.experimental.pallas import tpu as pltpu
from jax.sharding import Mesh
from jax.sharding import PartitionSpec as P

BOTTOM = 6
ALL = ("gx", "gy", "gz_0", "gz_1")
YZ = ("gy", "gz_0", "gz_1")
GZ = ("gz_0", "gz_1")
LANES = 128
WIDTH = 8
COUNT_Y = 4
COUNT_Z = 16
COLUMNS = COUNT_Y * COUNT_Z
SIZES = (48, 24, 12, 6)
CHUNK = 24

theta = 1.125
delta = 0.875
sigma = theta / delta
rho_0 = 1.0 / sigma
rho_1 = 1.0 / (2.0 * sigma - rho_0)
rho_2 = 1.0 / (2.0 * sigma - rho_1)
FIRST = (0.0, 1.0 / theta)
LATER = ((rho_1 * rho_0, 2.0 * rho_1 / delta), (rho_2 * rho_1, 2.0 * rho_2 / delta))

vmem = pl.BlockSpec(memory_space=pltpu.VMEM)
anywhere = pl.BlockSpec(memory_space=pl.ANY)


def roll(value, by, axis):
    axis = axis % value.ndim
    by = by % value.shape[axis]
    return pltpu.roll(value, by, axis) if by else value


def iota(shape, dim):
    return lax.broadcasted_iota(jnp.int32, shape, dim % len(shape))


def exact_dot(left, right):
    return jnp.dot(
        left, right, precision=lax.Precision.HIGHEST, preferred_element_type=jnp.float32
    )


class Wrapped:
    @staticmethod
    def low_y(v):
        return roll(v, 1, -2)

    @staticmethod
    def up_y(v):
        return roll(v, -1, -2)

    @staticmethod
    def low_z(v):
        return roll(v, 1, -1)

    @staticmethod
    def up_z(v):
        return roll(v, -1, -1)


class Columns:
    def __init__(self, cells):
        self.cells = cells

    def low_y(self, v):
        lane = iota(v.shape, -1)
        last = lax.slice_in_dim(v, self.cells - 1, self.cells, axis=v.ndim - 3)
        rest = lax.slice_in_dim(v, 0, self.cells - 1, axis=v.ndim - 3)
        lane = iota(last.shape, -1)
        last = jnp.where((lane >= COUNT_Z) & (lane < COLUMNS), roll(last, COUNT_Z, -1), 0.0)
        return jnp.concatenate([last, rest], axis=v.ndim - 3)

    def up_y(self, v):
        first = lax.slice_in_dim(v, 0, 1, axis=v.ndim - 3)
        rest = lax.slice_in_dim(v, 1, self.cells, axis=v.ndim - 3)
        lane = iota(first.shape, -1)
        first = jnp.where(lane < COLUMNS - COUNT_Z, roll(first, -COUNT_Z, -1), 0.0)
        return jnp.concatenate([rest, first], axis=v.ndim - 3)

    def low_z(self, v):
        lane, row = iota(v.shape, -1), iota(v.shape, -2)
        edge = roll(roll(v, 1 - self.cells, -2), 1, -1)
        edge = jnp.where((lane % COUNT_Z != 0) & (lane < COLUMNS), edge, 0.0)
        return jnp.where(row == 0, edge, roll(v, 1, -2))

    def up_z(self, v):
        lane, row = iota(v.shape, -1), iota(v.shape, -2)
        edge = roll(roll(v, self.cells - 1, -2), -1, -1)
        edge = jnp.where((lane % COUNT_Z != COUNT_Z - 1) & (lane < COLUMNS), edge, 0.0)
        inner = jnp.where(row < self.cells - 1, roll(v, -1, -2), 0.0)
        return jnp.where(row == self.cells - 1, edge, inner)


def set_up(stack, weight, planes, move):
    stack[1, planes] = stack[1, 0]

    def body(i, carry):
        cell, face_y, face_z = stack[4, i], stack[2, i], stack[3, i]
        total = stack[1, i] + stack[1, i + 1] + face_y + move.up_y(face_y)
        total = total + face_z + move.up_z(face_z)
        stack[5, i] = jnp.where(cell > 0.0, 1.0 / (cell + weight * total), 0.0)
        return carry

    lax.fori_loop(0, planes, body, 0)


def from_zero(stack, iterate, update, planes):
    def body(i, carry):
        step = FIRST[1] * (stack[5, i] * stack[0, i])
        update[i] = step
        iterate[i] = step
        return carry

    lax.fori_loop(0, planes, body, 0)


def stencil_pass(stack, iterate, weight, planes, count, move, use, carry):
    flux = stack[1, 0] * (iterate[0] - iterate[planes - 1])

    def body(i, both):
        flux, carry = both
        v = iterate[i]
        above = stack[1, i + 1] * (iterate[i + 1] - v)
        flux_y = stack[2, i] * (v - move.low_y(v))
        flux_z = stack[3, i] * (v - move.low_z(v))
        total = (flux - above) + (flux_y - move.up_y(flux_y)) + (flux_z - move.up_z(flux_z))
        carry = use(i, v, stack[0, i] - (stack[4, i] * v + weight * total), carry)
        return above, carry

    return lax.fori_loop(0, count, body, (flux, carry))[1]


def sweep(stack, iterate, update, weight, planes, move, factors):
    keep, gain = factors
    iterate[planes] = iterate[0]

    def use(i, v, remainder, carry):
        step = gain * (stack[5, i] * remainder)
        if keep:
            step = keep * update[i] + step
        update[i] = step
        iterate[i] = v + step
        return carry

    stencil_pass(stack, iterate, weight, planes, planes, move, use, 0)


def down(stack, iterate, update, weight, planes, move):
    from_zero(stack, iterate, update, planes)
    for factors in LATER:
        sweep(stack, iterate, update, weight, planes, move, factors)


def up(stack, iterate, update, weight, planes, move):
    for factors in (FIRST,) + LATER:
        sweep(stack, iterate, update, weight, planes, move, factors)


def keep_remainder(stack, iterate, update, weight, planes, count, move):
    iterate[planes] = iterate[0]

    def use(i, v, remainder, carry):
        update[i] = remainder
        return carry

    stencil_pass(stack, iterate, weight, planes, count, move, use, 0)


def coarsen(stack, remainder, rows, pairs, out, count, size):
    half = size // 2

    def body(i, carry):
        for k in range(5):
            if k == 1:
                rows[k] = stack[1, 2 * i]
            elif k == 0:
                rows[k] = remainder[2 * i] + remainder[2 * i + 1]
            else:
                rows[k] = stack[k, 2 * i] + stack[k, 2 * i + 1]
        for k in range(5):
            pair = rows[k, pl.ds(0, half, stride=2), :]
            if k != 2:
                pair = pair + rows[k, pl.ds(1, half, stride=2), :]
            pairs[k, i, 0:half, :] = pair
        return carry

    if half % 8:
        pairs[...] = jnp.zeros(pairs.shape, jnp.float32)
    lax.fori_loop(0, count // 2, body, 0)
    fine, coarse = iota((LANES, LANES), 0), iota((LANES, LANES), 1)
    mean = jnp.where((fine // 2 == coarse) & (fine < size), 1.0, 0.0)
    even = jnp.where((fine == 2 * coarse) & (fine < size), 1.0, 0.0)
    _, planes, padded, _ = pairs.shape
    for k in range(5):
        flat = pairs[k].reshape(planes * padded, LANES)
        scale = 0.125 if k in (0, 4) else 0.25
        made = scale * exact_dot(flat, even if k == 3 else mean)
        out(k, made.reshape(planes, padded, LANES))


def spread(coarse, spare, rows, fine, row_map, plane_maps):
    planes, height, _ = spare.shape
    source, target = iota((LANES, LANES), 0), iota((LANES, LANES), 1)
    half = target // 2
    pick = jnp.where(source == jnp.where(target < LANES // 2, half, LANES // 2 + half), 1.0, 0.0)
    wide = exact_dot(coarse[0:planes].reshape(planes * height, LANES), pick)
    spare[...] = wide.reshape(planes, height, LANES)
    rows[...] = jnp.zeros(rows.shape, jnp.float32)
    for count, plane_of, target_of in plane_maps:

        def body(i, carry):
            plane = plane_of(i)
            for start, number, first in row_map:
                part = spare[plane, start : start + number, :]
                rows[pl.ds(first, number, stride=2), :] = part
                rows[pl.ds(first + 1, number, stride=2), :] = part
            both = rows[...]
            at = target_of(i)
            fine[at] = fine[at] + both
            fine[at + 1] = fine[at + 1] + both
            return carry

        lax.fori_loop(0, count, body, 0)


def places():
    gx = lax.axis_index("gx")
    gy = lax.axis_index("gy")
    gz = lax.axis_index("gz_0") * 4 + lax.axis_index("gz_1")
    return gx, gy, gz


def widen(value):
    rows, lanes = value.shape
    if lanes == LANES:
        return value
    return jnp.concatenate([value, jnp.zeros((rows, LANES - lanes), jnp.float32)], axis=1)


def y_pack(parts, size):
    lane = iota((8, LANES), 1)
    tiles = [jnp.zeros((8, LANES), jnp.float32) for _ in range(-(-5 * size // LANES))]
    for k, part in enumerate(parts):
        start = k * size
        moved = roll(part, start % LANES, -1)
        for t in range(len(tiles)):
            a, b = max(start, t * LANES) - t * LANES, min(start + size, (t + 1) * LANES) - t * LANES
            if a < b:
                tiles[t] = jnp.where((lane >= a) & (lane < b), moved, tiles[t])
    return tiles


def y_unpack(tiles, k, size):
    lane = iota((8, LANES), 1)
    start = k * size
    t = start // LANES
    value = tiles[t]
    if start + size > (t + 1) * LANES:
        value = jnp.where(lane >= start - t * LANES, value, tiles[t + 1])
    return roll(value, -start, -1)


def pack(own, beside, size, outs):
    y_even, y_odd, z_even, z_odd, ee, eo, oe, oo = outs
    _, gy, gz = places()
    even_y, even_z = gy % 2 == 0, gz % 2 == 0
    lane = iota((size, LANES), 1)

    def group(g, slots, get):
        top = jnp.zeros((size, LANES), jnp.float32)
        bottom = top
        for s in range(slots):
            high, low = [], []
            for k in range(5):
                v = get(k, s)
                at = 40 * s + 8 * k
                here = (lane >= at) & (lane < at + 8)
                top = jnp.where(here, roll(v, at - (size - 8), -1), top)
                bottom = jnp.where(here, roll(v, at, -1), bottom)
                high.append(v[size - 8 :])
                low.append(v[:8])
            for t, (h, l) in enumerate(zip(y_pack(high, size), y_pack(low, size))):
                y_even[3 * g + s, 8 * t : 8 * t + 8, :] = jnp.where(even_y, h, l)
                y_odd[3 * g + s, 8 * t : 8 * t + 8, :] = jnp.where(even_y, l, h)
        a, b = jnp.where(even_z, top, bottom), jnp.where(even_z, bottom, top)
        z_even[g] = a
        z_odd[g] = b
        ee[g] = jnp.where(even_y, a[size - 8 :], a[:8])
        eo[g] = jnp.where(even_y, b[size - 8 :], b[:8])
        oe[g] = jnp.where(even_y, a[:8], a[size - 8 :])
        oo[g] = jnp.where(even_y, b[:8], b[size - 8 :])

    def body(g, carry):
        group(g, 3, lambda k, s: own(k, 3 * g + s))
        return carry

    lax.fori_loop(0, size // 3, body, 0)
    for q in range(3):
        group(size // 3 + q, min(3, 8 - 3 * q), lambda k, s: beside(k, 3 * q + s))


def unpack(stack, own, beside, size, payloads):
    y_even, y_odd, z_even, z_odd, ee, eo, oe, oo = payloads
    gx, gy, gz = places()
    even_y, even_z = gy % 2 == 0, gz % 2 == 0
    lane, lane_8 = iota((size, LANES), 1), iota((8, LANES), 1)
    tiles = -(-5 * size // LANES)

    def join(lane, middle, low, high, at):
        sides = jnp.where(lane >= LANES - 8, roll(low, LANES - 8 - at, -1), 0.0)
        sides = jnp.where(lane < size + 8, roll(high, size - at, -1), sides)
        return jnp.where(lane < size, middle, sides)

    def group(g, slots, get, first):
        low = jnp.where(even_z, z_odd[g], z_even[g])
        high = jnp.where(even_z, z_even[g], z_odd[g])
        by_even = jnp.where(even_z, eo[g], ee[g]), jnp.where(even_z, ee[g], eo[g])
        by_odd = jnp.where(even_z, oo[g], oe[g]), jnp.where(even_z, oe[g], oo[g])
        corners = (
            [jnp.where(even_y, e, o) for e, o in zip(by_even, by_odd)],
            [jnp.where(even_y, o, e) for e, o in zip(by_even, by_odd)],
        )
        for s in range(slots):
            e, o = y_even[3 * g + s], y_odd[3 * g + s]
            ends = jnp.where(even_y, e, o), jnp.where(even_y, o, e)
            ends = [[end[8 * t : 8 * t + 8] for t in range(tiles)] for end in ends]
            for k in range(5):
                at = 40 * s + 8 * k
                stack[k, first + s, 0:size, :] = join(lane, get(k, s), low, high, at)
                for which in range(2):
                    rows = slice(size + 8 * which, size + 8 * which + 8)
                    middle = y_unpack(ends[which], k, size)
                    stack[k, first + s, rows, :] = join(lane_8, middle, *corners[which], at)

    def body(g, carry):
        group(g, 3, lambda k, s: own(k, 3 * g + s), 3 * g)
        return carry

    lax.fori_loop(0, size // 3, body, 0)
    for q in range(3):
        group(
            size // 3 + q,
            min(3, 8 - 3 * q),
            lambda k, s: beside(k, 3 * q + s),
            size + gx + 3 * q,
        )
    empty = size + 8 * (1 - gx)
    for k in range(5):
        stack[k, empty] = jnp.zeros(stack.shape[2:], jnp.float32)


def payload_shapes(size):
    groups = size // 3 + 3
    tall = 8 * (-(-5 * size // LANES))
    y = jax.ShapeDtypeStruct((size + 8, tall, LANES), jnp.float32)
    z = jax.ShapeDtypeStruct((groups, size, LANES), jnp.float32)
    c = jax.ShapeDtypeStruct((groups, 8, LANES), jnp.float32)
    return [y, y, z, z, c, c, c, c]


def partner(index, parity, count):
    if parity is None:
        return index
    other = index + 1 if index % 2 == parity else index - 1
    return other if 0 <= other < count else None


def swap(value, parity_y, parity_z):
    pairs = []
    for y in range(COUNT_Y):
        for z in range(COUNT_Z):
            to_y, to_z = partner(y, parity_y, COUNT_Y), partner(z, parity_z, COUNT_Z)
            if to_y is not None and to_z is not None:
                pairs.append((y * COUNT_Z + z, to_y * COUNT_Z + to_z))
    return lax.ppermute(value, YZ, pairs)


WAYS = ((0, None), (1, None), (None, 0), (None, 1), (0, 0), (0, 1), (1, 0), (1, 1))


def swap_cores(value):
    return lax.ppermute(value, "gx", [(0, 1), (1, 0)])


def f32(*shape):
    return jax.ShapeDtypeStruct(shape, jnp.float32)


def call(body, outs, ins, scratch, operands):
    return pl.pallas_call(
        body,
        out_shape=[shape for shape, _ in outs],
        out_specs=[spec for _, spec in outs],
        in_specs=ins,
        scratch_shapes=scratch,
        compiler_params=pltpu.CompilerParams(vmem_limit_bytes=56 * 2**20),
    )(*operands)


def edge_kernel(right, faces, cells, out, sems):
    gx = lax.axis_index("gx")
    start = (1 - gx) * (SIZES[0] - WIDTH)
    part = pl.ds(start, WIDTH)
    copies = [
        pltpu.make_async_copy(right.at[part], out.at[0], sems.at[0]),
        pltpu.make_async_copy(faces.at[0, part], out.at[1], sems.at[1]),
        pltpu.make_async_copy(faces.at[1, part], out.at[2], sems.at[2]),
        pltpu.make_async_copy(faces.at[2, part], out.at[3], sems.at[3]),
        pltpu.make_async_copy(cells.at[part], out.at[4], sems.at[4]),
    ]
    for copy in copies:
        copy.start()
    for copy in copies:
        copy.wait()


def own_inputs(right, faces, cells):
    def own(k, i):
        if k == 0:
            return widen(right[i])
        return widen(cells[i] if k == 4 else faces[k - 1, i])

    return own


def pack_0_kernel(right, faces, cells, beside, *outs):
    pack(own_inputs(right, faces, cells), lambda k, j: widen(beside[k, j]), SIZES[0], outs)


def pack_1_kernel(own, beside, *outs):
    pack(lambda k, i: own[k, i], lambda k, j: beside[k, j], SIZES[1], outs)


def start_kept(stack, kept, sem):
    copy = pltpu.make_async_copy(stack, kept, sem)
    copy.start()
    return copy


def level_0_kernel(
    right, faces, cells, beside, ye, yo, ze, zo, ee, eo, oe, oo,
    coarse, coarse_edge, kept_stack, kept_iterate,
    stack, iterate, update, rows, pairs, sems,
):
    size = SIZES[0]
    planes = size + 9
    gx = lax.axis_index("gx")
    unpack(
        stack,
        own_inputs(right, faces, cells),
        lambda k, j: widen(beside[k, j]),
        size,
        (ye, yo, ze, zo, ee, eo, oe, oo),
    )
    set_up(stack, 1.0, planes, Wrapped)
    first = start_kept(stack, kept_stack, sems.at[0])
    down(stack, iterate, update, 1.0, planes, Wrapped)
    own = pl.ds(0, planes)
    keep_remainder(stack, iterate, update, 1.0, planes, size, Wrapped)
    second = start_kept(iterate.at[own], kept_iterate.at[own], sems.at[1])

    def out(k, value):
        coarse[k] = value
        coarse_edge[k] = jnp.where(gx == 0, value[16:24], value[0:8])

    coarsen(stack, update, rows, pairs, out, size, size)
    first.wait()
    second.wait()


def level_1_kernel(
    own, beside, ye, yo, ze, zo, ee, eo, oe, oo,
    coarse, kept_stack, kept_iterate,
    stack, iterate, update, rows, pairs, made, sems,
):
    size = SIZES[1]
    planes = size + 9
    gx = lax.axis_index("gx")
    unpack(
        stack,
        lambda k, i: own[k, i],
        lambda k, j: beside[k, j],
        size,
        (ye, yo, ze, zo, ee, eo, oe, oo),
    )
    set_up(stack, 0.25, planes, Wrapped)
    first = start_kept(stack, kept_stack, sems.at[0])
    down(stack, iterate, update, 0.25, planes, Wrapped)
    keep_remainder(stack, iterate, update, 0.25, planes, size, Wrapped)
    inside = pl.ds(0, planes)
    second = start_kept(iterate.at[inside], kept_iterate.at[inside], sems.at[1])

    def out(k, value):
        made[k] = value

    coarsen(stack, update, rows, pairs, out, size, size)
    for i in range(SIZES[2]):
        line = made[0, i]
        for k in range(1, 5):
            line = line + roll(made[k, i], SIZES[2] * k, -1)
        coarse[i] = jnp.where(gx == 0, line, roll(line, LANES // 2, -1))
    first.wait()
    second.wait()


def level_2_kernel(
    own, ye, yo, ze, zo, ee, eo, oe, oo,
    payload, kept_stack, kept_iterate,
    stack, iterate, update, rows, pairs, made, lines, sems,
):
    size = SIZES[2]
    planes = 2 * size + 1
    _, gy, gz = places()
    even_y, even_z = gy % 2 == 0, gz % 2 == 0
    lane = iota((16, LANES), 1)
    bases = (0, size, LANES - size)
    for k in range(5):
        stack[k, 2 * size] = jnp.zeros(stack.shape[2:], jnp.float32)

    def body(i, carry):
        e = ee[i], eo[i]
        o = oe[i], oo[i]
        table = (
            (own[i], jnp.where(even_z, ze[i], zo[i]), jnp.where(even_z, zo[i], ze[i])),
            (
                jnp.where(even_y, ye[i], yo[i]),
                jnp.where(even_y, jnp.where(even_z, e[0], e[1]), jnp.where(even_z, o[0], o[1])),
                jnp.where(even_y, jnp.where(even_z, e[1], e[0]), jnp.where(even_z, o[1], o[0])),
            ),
            (
                jnp.where(even_y, yo[i], ye[i]),
                jnp.where(even_y, jnp.where(even_z, o[0], o[1]), jnp.where(even_z, e[0], e[1])),
                jnp.where(even_y, jnp.where(even_z, o[1], o[0]), jnp.where(even_z, e[1], e[0])),
            ),
        )
        for k in range(5):
            for h in range(2):
                source = (LANES // 2) * h + size * k
                plane = size * h + i
                stack[k, plane, 24:32, :] = jnp.zeros((8, LANES), jnp.float32)
                for a, first in enumerate((0, size, 40 - size)):
                    line = jnp.zeros((16, LANES), jnp.float32)
                    for b, base in enumerate(bases):
                        here = (lane >= base) & (lane < base + size)
                        line = jnp.where(here, roll(table[a][b], base - source, -1), line)
                    stack[k, plane, first : first + size, :] = line[:size]
        return carry

    lax.fori_loop(0, size, body, 0)
    weight = 0.0625
    set_up(stack, weight, planes, Wrapped)
    first = start_kept(stack, kept_stack, sems.at[0])
    down(stack, iterate, update, weight, planes, Wrapped)
    keep_remainder(stack, iterate, update, weight, planes, 2 * size, Wrapped)
    inside = pl.ds(0, planes)
    second = start_kept(iterate.at[inside], kept_iterate.at[inside], sems.at[1])

    def out(k, value):
        made[k * 96 : k * 96 + 96, :] = value.reshape(96, LANES)

    coarsen(stack, update, rows, pairs, out, 2 * size, size)
    line = jnp.zeros((60, LANES), jnp.float32)
    for y in range(6):
        line = line + roll(made[pl.ds(y, 60, stride=8), :], 6 * y, -1)
    lines[0:60, :] = line
    chunk = lines[0:20, :] + roll(lines[20:40, :], 40, -1) + roll(lines[40:60, :], 80, -1)
    chunk = jnp.concatenate([chunk, jnp.zeros((4, LANES), jnp.float32)], axis=0)

    def repeat(c, carry):
        payload[pl.ds(pl.multiple_of(c * CHUNK, 8), CHUNK), :] = chunk
        return carry

    lax.fori_loop(0, COLUMNS, repeat, 0)
    first.wait()
    second.wait()


def compact(value):
    row = iota(value.shape, -2)
    out = jnp.where(row == 0, value, 0.0)
    out = jnp.where(row == 1, roll(value, -1, -2), out)
    return jnp.where(row == 2, roll(value, -2, -2), out)


def bottom(source, faces, cells):
    weight = 0.25**4
    move = Columns(3)
    face_x, face_y, face_z = faces
    nothing = jnp.zeros((1,) + source.shape[1:], jnp.float32)

    def apply(v):
        flux_x = face_x * (v - jnp.concatenate([nothing, v[:-1]], axis=0))
        flux_y = face_y * (v - move.low_y(v))
        flux_z = face_z * (v - move.low_z(v))
        total = flux_x - jnp.concatenate([flux_x[1:], nothing], axis=0)
        total = total + (flux_y - move.up_y(flux_y)) + (flux_z - move.up_z(flux_z))
        return cells * v + weight * total

    def total_of(v):
        flat = jnp.sum(jnp.sum(v, axis=0), axis=0)
        one = jnp.sum(jnp.sum(flat, axis=0, keepdims=True), axis=1, keepdims=True)
        return jnp.broadcast_to(one, flat.shape)

    iterate = jnp.zeros_like(source)
    remainder = source
    search = source
    norm_now = total_of(remainder * remainder)
    for step in range(BOTTOM):
        applied = apply(search)
        size = norm_now / total_of(search * applied)
        iterate = iterate + size * search
        if step + 1 < BOTTOM:
            remainder = remainder - size * applied
            norm_next = total_of(remainder * remainder)
            search = remainder + (norm_next / norm_now) * search
            norm_now = norm_next
    return iterate


def rise_kernel(
    gathered, stack_2_in, iterate_2_in, stack_1_in, iterate_1_in, stack_0_in, iterate_0_in,
    solution_out, residual_out, sums,
    stack_0, iterate_0, update_0, rows_0, spare_1,
    stack_1, iterate_1, update_1, rows_1, spare_2,
    stack_2, iterate_2, update_2, rows_2, spare_3,
    stack_3, iterate_3, update_3, turned, table, block_3, sems,
):
    gx, gy, gz = places()
    loads = []
    for n, (source, target) in enumerate(
        (
            (stack_2_in, stack_2),
            (iterate_2_in, iterate_2),
            (stack_1_in, stack_1),
            (iterate_1_in, iterate_1),
            (stack_0_in, stack_0),
            (iterate_0_in, iterate_0),
        )
    ):
        copy = pltpu.make_async_copy(source, target, sems.at[n])
        copy.start()
        loads.append(copy)

    stack_3[...] = jnp.zeros(stack_3.shape, jnp.float32)
    blank = jnp.zeros((LANES - COLUMNS, LANES), jnp.float32)
    for r in range(20):
        part = gathered[pl.ds(r, COLUMNS, stride=CHUNK), :]
        turned[...] = jnp.transpose(jnp.concatenate([part, blank], axis=0))
        for j in range(3):
            k, x = divmod(20 * j + r, 12)
            for y in range(6):
                stack_3[k, x, y, 0:6, :] = turned[40 * j + 6 * y : 40 * j + 6 * y + 6, :]
    move = Columns(6)
    weight = 0.25**3
    set_up(stack_3, weight, 13, move)
    down(stack_3, iterate_3, update_3, weight, 13, move)
    keep_remainder(stack_3, iterate_3, update_3, weight, 13, 12, move)

    def coarse(k, x_pair, y_pair, z_pair, scale):
        planes = []
        for x in range(6):
            read = (lambda i: update_3[i]) if k == 0 else (lambda i: stack_3[k, i])
            v = read(2 * x)
            if x_pair:
                v = v + read(2 * x + 1)
            lines = []
            for y in range(3):
                line = v[2 * y]
                if y_pair:
                    line = line + v[2 * y + 1]
                if z_pair:
                    line = line + roll(line, -1, -2)
                lines.append(scale * compact(line))
            planes.append(jnp.stack(lines))
        return jnp.stack(planes)

    lowest = bottom(
        coarse(0, True, True, True, 0.125),
        (
            coarse(1, False, True, True, 0.25),
            coarse(2, True, False, True, 0.25),
            coarse(3, True, True, False, 0.25),
        ),
        coarse(4, True, True, True, 0.125),
    )
    row = iota((8, LANES), 0)
    for x in range(6):
        for y in range(3):
            line = lowest[x, y]
            wide = jnp.where(row == 0, line, 0.0)
            for to in range(1, 6):
                wide = jnp.where(row == to, roll(line, to - to // 2, -2), wide)
            for a in range(2):
                for b in range(2):
                    iterate_3[2 * x + a, 2 * y + b] = iterate_3[2 * x + a, 2 * y + b] + wide
    up(stack_3, iterate_3, update_3, weight, 13, move)

    low_rows = jnp.zeros((32, LANES), jnp.float32)
    for q in range(6):
        two = [iterate_3[2 * q + h].reshape(48, LANES) for h in range(2)]
        table[q] = jnp.transpose(jnp.concatenate(two + [low_rows], axis=0))
    block_3[...] = jnp.zeros(block_3.shape, jnp.float32)
    lane = iota((8, LANES), 1)

    def place(q, carry):
        for a, first in ((0, 0), (1, 6), (-1, 18)):
            lines = [jnp.zeros((8, LANES), jnp.float32) for _ in range(2)]
            for b, base in ((0, 0), (1, 6), (-1, LANES - 6)):
                y, z = gy + a, gz + b
                inside = (y >= 0) & (y < COUNT_Y) & (z >= 0) & (z < COUNT_Z)
                at = jnp.where(inside, y * COUNT_Z + z, 0)
                here = (lane >= base) & (lane < base + 6) & inside
                found = jnp.broadcast_to(table[q, pl.ds(at, 1), :], (8, LANES))
                for h in range(2):
                    for y_in in range(6):
                        moved = roll(found, base - 48 * h - 8 * y_in, -1)
                        lines[h] = jnp.where(here & (row == y_in), moved, lines[h])
            for h in range(2):
                block_3[2 * q + h, first : first + 6, :] = lines[h][0:6]
        return carry

    lax.fori_loop(0, 6, place, 0)

    loads[0].wait()
    loads[1].wait()
    spread(
        block_3, spare_3, rows_2, iterate_2,
        ((0, 12, 0), (18, 6, 28)),
        ((12, lambda i: i, lambda i: 2 * i),),
    )
    up(stack_2, iterate_2, update_2, 0.0625, 25, Wrapped)

    loads[2].wait()
    loads[3].wait()
    size = SIZES[1]
    spread(
        iterate_2, spare_2, rows_1, iterate_1,
        ((0, 16, 0), (36, 4, 32)),
        (
            (12, lambda i: 12 * gx + i, lambda i: 2 * i),
            (4, lambda i: 12 - 4 * gx + i, lambda i: size + gx + 2 * i),
        ),
    )
    up(stack_1, iterate_1, update_1, 0.25, size + 9, Wrapped)

    loads[4].wait()
    loads[5].wait()
    size = SIZES[0]
    spread(
        iterate_1, spare_1, rows_0, iterate_0,
        ((0, 28, 0), (36, 4, 56)),
        (
            (24, lambda i: i, lambda i: 2 * i),
            (4, lambda i: 24 + 5 * gx + i, lambda i: size + gx + 2 * i),
        ),
    )
    planes = size + 9
    up(stack_0, iterate_0, update_0, 1.0, planes, Wrapped)
    iterate_0[planes] = iterate_0[0]
    mask = iota((size, LANES), 1) < size

    def use(i, v, remainder, carry):
        solution_out[i] = v[0:size, 0:size]
        residual_out[i] = remainder[0:size, 0:size]
        mine = jnp.where(mask, remainder[0:size], 0.0)
        given = jnp.where(mask, stack_0[0, i, 0:size, :], 0.0)
        return carry[0] + mine * mine, carry[1] + given * given

    zero = jnp.zeros((size, LANES), jnp.float32)
    squares = stencil_pass(stack_0, iterate_0, 1.0, planes, size, Wrapped, use, (zero, zero))
    ones = []
    for square in squares:
        one = jnp.sum(jnp.sum(square, axis=0, keepdims=True), axis=1, keepdims=True)
        ones.append(jnp.broadcast_to(one, (8, LANES)))
    sums[...] = jnp.where(lane == 0, ones[0], jnp.where(lane == 1, ones[1], 0.0))


def shards(right, faces, cells):
    dma = pltpu.SemaphoreType.DMA
    buf = lambda *shape: pltpu.VMEM(shape, jnp.float32)
    edge = call(
        edge_kernel,
        [(f32(5, WIDTH, 48, 48), anywhere)],
        [anywhere] * 3,
        [dma((5,))],
        (right, faces, cells),
    )[0]
    beside = swap_cores(edge)
    outs = call(
        pack_0_kernel,
        [(s, vmem) for s in payload_shapes(48)],
        [vmem] * 4,
        [],
        (right, faces, cells, beside),
    )
    moved = [swap(v, *way) for v, way in zip(outs, WAYS)]
    coarse, coarse_edge, stack_0, iterate_0 = call(
        level_0_kernel,
        [
            (f32(5, 24, 24, LANES), vmem),
            (f32(5, WIDTH, 24, LANES), vmem),
            (f32(6, 58, 64, LANES), anywhere),
            (f32(58, 64, LANES), anywhere),
        ],
        [vmem] * 12,
        [
            buf(6, 58, 64, LANES),
            buf(58, 64, LANES),
            buf(58, 64, LANES),
            buf(5, 64, LANES),
            buf(5, 24, 24, LANES),
            dma((2,)),
        ],
        (right, faces, cells, beside, *moved),
    )
    beside = swap_cores(coarse_edge)
    outs = call(
        pack_1_kernel,
        [(s, vmem) for s in payload_shapes(24)],
        [vmem] * 2,
        [],
        (coarse, beside),
    )
    moved = [swap(v, *way) for v, way in zip(outs, WAYS)]
    coarse, stack_1, iterate_1 = call(
        level_1_kernel,
        [
            (f32(12, 16, LANES), vmem),
            (f32(6, 34, 40, LANES), anywhere),
            (f32(34, 40, LANES), anywhere),
        ],
        [vmem] * 10,
        [
            buf(6, 34, 40, LANES),
            buf(34, 40, LANES),
            buf(34, 40, LANES),
            buf(5, 40, LANES),
            buf(5, 12, 16, LANES),
            buf(5, 12, 16, LANES),
            dma((2,)),
        ],
        (coarse, beside, *moved),
    )
    coarse = coarse + swap_cores(coarse)
    moved = [swap(coarse, *way) for way in WAYS]
    payload, stack_2, iterate_2 = call(
        level_2_kernel,
        [
            (f32(COLUMNS * CHUNK, LANES), vmem),
            (f32(6, 26, 40, LANES), anywhere),
            (f32(26, 40, LANES), anywhere),
        ],
        [vmem] * 9,
        [
            buf(6, 26, 40, LANES),
            buf(26, 40, LANES),
            buf(26, 40, LANES),
            buf(5, 40, LANES),
            buf(5, 12, 8, LANES),
            buf(480, LANES),
            buf(64, LANES),
            dma((2,)),
        ],
        (coarse, *moved),
    )
    payload = payload.reshape(COLUMNS, CHUNK, LANES)
    gathered = lax.all_to_all(payload, YZ, 0, 0).reshape(COLUMNS * CHUNK, LANES)
    solved, residual, sums = call(
        rise_kernel,
        [(f32(48, 48, 48), vmem), (f32(48, 48, 48), vmem), (f32(8, LANES), vmem)],
        [vmem] + [anywhere] * 6,
        [
            buf(6, 58, 64, LANES), buf(58, 64, LANES), buf(58, 64, LANES), buf(64, LANES),
            buf(33, 40, LANES),
            buf(6, 34, 40, LANES), buf(34, 40, LANES), buf(34, 40, LANES), buf(40, LANES),
            buf(24, 40, LANES),
            buf(6, 26, 40, LANES), buf(26, 40, LANES), buf(26, 40, LANES), buf(40, LANES),
            buf(12, 24, LANES),
            buf(6, 14, 6, 8, LANES), buf(14, 6, 8, LANES), buf(14, 6, 8, LANES),
            buf(LANES, LANES), buf(6, LANES, LANES), buf(12, 24, LANES),
            dma((6,)),
        ],
        (gathered, stack_2, iterate_2, stack_1, iterate_1, stack_0, iterate_0),
    )
    each = jnp.broadcast_to(sums[0:1].reshape(1, 1, LANES), (128, 1, LANES))
    total = jnp.sum(lax.all_to_all(each, ALL, 0, 0), axis=(0, 1))
    return solved, residual, jnp.sqrt(total[0] / total[1])


def solution(mesh):
    torus = Mesh(
        mesh.devices.reshape(mesh.shape["gx"], mesh.shape["gy"], 4, 4), ("gx", "gy", "gz_0", "gz_1")
    )
    in_specs = (P("gx", "gy", GZ), P(None, "gx", "gy", GZ), P("gx", "gy", GZ))
    out_specs = (P("gx", "gy", GZ), P("gx", "gy", GZ), P())
    return jax.shard_map(
        shards, mesh=torus, in_specs=in_specs, out_specs=out_specs, check_vma=False
    )
```

time: 1260 us -> 370 us (0.29); the launches traced: 1230 us -> 367 us
  local copies, waits for them, and re-layouts: 370 us -> 6.86 us
  starting transfers between devices: 433 us -> 80.5 us
  other arithmetic: 232 us -> 0.94 us
  Pallas kernels: 0 us -> 213 us
  blocking collectives: 119 us -> 38.3 us
  between operations: 35 us -> 3.73 us
  waiting for transfers between devices: 45.4 us -> 24 us
    ppermute x165 -> x27, starting transfers between devices: 433 us -> 80.5 us  [the longest x24 80.2 us: swap(): return lax.ppermute(value, YZ, pairs)]
    pallas_call x0 -> x7, Pallas kernels: none -> 213 us  [call(): pl.pallas_call(body, out_shape=[shape for shape, _ in outs], out_specs=[s...]
    reduce_sum x33 -> x1, other arithmetic: 115 us -> 0.03 us  [shards(): total = jnp.sum(lax.all_to_all(each, ALL, 0, 0), axis=(0, 1))]
    slice x111 -> x1, local copies, waits for them, and re-layouts: 104 us -> 0.59 us  [shards(): return (solved, residual, jnp.sqrt(total[0] / total[1]))]
    add x30 -> x1, other arithmetic: 80.5 us -> 0.91 us  [shards(): coarse = coarse + swap_cores(coarse)]
    unnamed x1 -> x0, blocking collectives: 76.1 us -> none
    reshape x12 -> x0, local copies, waits for them, and re-layouts: 71.8 us -> none  [the longest x5 38.3 us: average_cells(): field.reshape(field.shape[0] // 2, 2, field.shape[1] // 2, 2, field.shape...]
    another operation x13 -> x0, local copies, waits for them, and re-layouts: 71.1 us -> none  [the longest x4 23.3 us: average_faces(): along_z = faces[2].reshape(halves)[..., 0]]
  transfers between devices with their start and end apart: 166 -> 27, of which waited for: 26 -> 8; matrix products, arithmetic and copies ran while one was open for 29% -> 0% of each run, Pallas kernels for 0% -> 0%
where the time goes in v1:
time: 370 us; the launch traced here: 367 us
  Pallas kernels  213 us (58%)
  starting transfers between devices  80.5 us (22%)
  blocking collectives  38.3 us (10%)
  waiting for transfers between devices  24 us (6%)
  local copies, waits for them, and re-layouts  6.86 us (2%)
  between operations  3.73 us (1%)
    pallas_call x7, Pallas kernels, call(): pl.pallas_call(body, out_shape=[shape for shape, _ in outs], out_specs=[s...  213 us
    ppermute x24, starting transfers between devices, swap(): return lax.ppermute(value, YZ, pairs)  80.2 us
    all_to_all x1, blocking collectives, shards(): gathered = lax.all_to_all(payload, YZ, 0, 0).reshape(COLUMNS * CHUNK, LANES)  24.7 us
    ppermute x24, waiting for transfers between devices, swap(): return lax.ppermute(value, YZ, pairs)  17.6 us
    all_to_all x1, blocking collectives, shards(): total = jnp.sum(lax.all_to_all(each, ALL, 0, 0), axis=(0, 1))  13.6 us
  transfers between devices with their start and end apart: 27, of which 8 were waited for; matrix products, arithmetic and copies ran while one was open for 0% of the time, Pallas kernels for 0%

profile of v1, /device:TPU:8, one launch (start us, length us, event | category | flops | bytes accessed | tf_op | source)
XLA Modules:
  0.0 367.4 jit_solution(1814073049523756159)
XLA Ops:
  0.6 30.9 %shard_map.58 = f32[5,8,48,48]{3,2,1,0:T(8,128)} custom-call(f32[48,48,48]{2,1,0:T(8,128)} %right.5, f32[3,48,48,48]{3,2,1,0:T(8,128)} %faces.5, f32[48,48,48]{2,1,0:T(8,128)} %cells.5), custom_call_target="tpu_custom_call" | custom-call | tf_op jit(solution)/shard_map/pallas_call | solution.py:399
  31.7 2.8 collective-permute-done.beside
  34.4 0.9 copy-done
  35.4 9.1 %shard_map.59 = (f32[56,16,128]{2,1,0:T(8,128)}, f32[56,16,128]{2,1,0:T(8,128)}, f32[19,48,128]{2,1,0:T(8,128)}, f32[19,48,128]{2,1,0:T(8,128)}, f32[19,8,128]{2...) custom-call(f32[48,48,48]{2,1,0:T(8,128)} %right.5, f32[3,48,48,48]{3,2,1,0:T(8,128)} %faces.5, ...), custom_call_target="tpu_custom_call" | custom-call | tf_op jit(solution)/shard_map/pallas_call | solution.py:399
  44.5 0.3 collective-permute-start.3
  44.8 4.5 %collective-permute-start.4 = (f32[19,48,128]{2,1,0:T(8,128)}, f32[19,48,128]{2,1,0:T(8,128)S(1)}, u32[]{:S(2)}, u32[]{:S(2)}) collective-permute-start(f32[19,48,128]{2,1,0:T(8,128)} %get-tuple-element.35), channel_id=1, source_target_pairs={{1,2},{2,1},{3,4},{4,3},{5,6},{6,5},{7,8},{8,7},{9,10},{10,9},{11,... | collective-permute-start | bytes 1400840 | tf_op jit(solution)/shard_map/ppermute | solution.py:384
  49.3 1.6 collective-permute-start.1
  50.9 0.7 collective-permute-start.2
  51.5 1.4 collective-permute-start.5
  52.9 9.3 %collective-permute-done.5.ee = f32[19,8,128]{2,1,0:T(8,128)S(1)} collective-permute-done((f32[19,8,128]{2,1,0:T(8,128)}, f32[19,8,128]{2,1,0:T(8,128)S(1)}, u32[]{:S(2)}, u32[]{:S(2)}) %collective-permute-start.5) | collective-permute-done | bytes 77856 | tf_op jit(solution)/shard_map/ppermute | solution.py:384
  62.2 6.4 %collective-permute-start.6 = (f32[19,8,128]{2,1,0:T(8,128)}, f32[19,8,128]{2,1,0:T(8,128)S(1)}, u32[]{:S(2)}, u32[]{:S(2)}) collective-permute-start(f32[19,8,128]{2,1,0:T(8,128)} %get-tuple-element.37), channel_id=1, source_target_pairs={{1,18},{2,17},{3,20},{4,19},{5,22},{6,21},{7,24},{8,23},{9,26},{10... | collective-permute-start | bytes 233480 | tf_op jit(solution)/shard_map/ppermute | solution.py:384
  68.7 2.6 collective-permute-done.6.eo
  71.2 0.7 collective-permute-start.7
  71.9 0.7 collective-permute-start.8
  72.7 0.5 copy-done.22
  73.3 0.2 copy-done.4
  73.5 0.2 copy-done.2
  73.7 0.8 copy-done.3
  74.5 43.1 %shard_map.60 = (f32[5,24,24,128]{3,2,1,0:T(8,128)}, f32[5,8,24,128]{3,2,1,0:T(8,128)}, f32[6,58,64,128]{3,2,1,0:T(8,128)}, f32[58,64,128]{2,1,0:T(8,128)}) custom-call(f32[48,48,48]{2,1,0:T(8,128)} %right.5, f32[3,48,48,48]{3,2,1,0:T(8,128)} %faces.5, f32[48,48,48]{2,1,0:T(8,128)} %cells.5, f32[5,8,48,48]{3,2,1,0:T(8,128)} %copy-done, ...), custom_call_target="tpu_custom_call" | custom-call | tf_op jit(solution)/shard_map/pallas_call | solution.py:399
  117.8 2.1 collective-permute-done.9.beside
  119.8 0.8 copy-done.1
  120.6 4.1 %shard_map.61 = (f32[32,8,128]{2,1,0:T(8,128)}, f32[32,8,128]{2,1,0:T(8,128)}, f32[11,24,128]{2,1,0:T(8,128)}, f32[11,24,128]{2,1,0:T(8,128)}, f32[11,8,128]{2,1...) custom-call(f32[5,24,24,128]{3,2,1,0:T(8,128)} %get-tuple-element.40.own, ...), custom_call_target="tpu_custom_call" | custom-call | tf_op jit(solution)/shard_map/pallas_call | solution.py:399
  124.7 7.4 %collective-permute-start.14 = (f32[11,8,128]{2,1,0:T(8,128)}, f32[11,8,128]{2,1,0:T(8,128)S(1)}, u32[]{:S(2)}, u32[]{:S(2)}) collective-permute-start(f32[11,8,128]{2,1,0:T(8,128)} %get-tuple-element.46), channel_id=1, source_target_pairs={{0,17},{1,16},{2,19},{3,18},{4,21},{5,20},{6,23},{7,22},{8,25},{9,... | collective-permute-start | bytes 135176 | tf_op jit(solution)/shard_map/ppermute | solution.py:384
  132.1 10.9 %collective-permute-start.15 = (f32[11,8,128]{2,1,0:T(8,128)}, f32[11,8,128]{2,1,0:T(8,128)S(1)}, u32[]{:S(2)}, u32[]{:S(2)}) collective-permute-start(f32[11,8,128]{2,1,0:T(8,128)} %get-tuple-element.47), channel_id=1, source_target_pairs={{1,18},{2,17},{3,20},{4,19},{5,22},{6,21},{7,24},{8,23},{9,26},{10... | collective-permute-start | bytes 135176 | tf_op jit(solution)/shard_map/ppermute | solution.py:384
  143.1 9.0 %collective-permute-start.13 = (f32[11,24,128]{2,1,0:T(8,128)}, f32[11,24,128]{2,1,0:T(8,128)S(1)}, u32[]{:S(2)}, u32[]{:S(2)}) collective-permute-start(f32[11,24,128]{2,1,0:T(8,128)} %get-tuple-element.45), channel_id=1, source_target_pairs={{1,2},{2,1},{3,4},{4,3},{5,6},{6,5},{7,8},{8,7},{9,10},{10,9},{11,... | collective-permute-start | bytes 405512 | tf_op jit(solution)/shard_map/ppermute | solution.py:384
  152.1 0.7 collective-permute-start.11
  152.8 0.7 collective-permute-start.16
  153.5 0.7 collective-permute-start.17
  154.2 3.1 collective-permute-done.10.ye
  157.4 0.6 copy-done.9
  158.0 0.7 copy-done.8
  158.7 22.3 %shard_map.62 = (f32[12,16,128]{2,1,0:T(8,128)}, f32[6,34,40,128]{3,2,1,0:T(8,128)}, f32[34,40,128]{2,1,0:T(8,128)}) custom-call(f32[5,24,24,128]{3,2,1,0:T(8,128)} %get-tuple-element.40.own, f32[5,8,24,128]{3,2,1,0:T(8,128)} %copy-done.1, f32[32,8,128]{2,1,0:T(8,128)} %copy-done.9, f32[32,8,128]{2,1,0:T(8,128)} %copy-done.10, f32[11,24,128]{2,1,0:T(8,128)} %copy-done.7, ...), custom_call_target="tpu_custom_call" | custom-call | tf_op jit(solution)/shard_map/pallas_call | solution.py:399
  181.1 1.5 collective-permute-done.18
  182.6 0.9 add.3.own
  183.5 0.7 collective-permute-start.26
  184.2 0.7 collective-permute-start.25
  184.9 25.4 %collective-permute-start.24 = (f32[12,16,128]{2,1,0:T(8,128)S(1)}, f32[12,16,128]{2,1,0:T(8,128)S(1)}, u32[]{:S(2)}, u32[]{:S(2)}) collective-permute-start(f32[12,16,128]{2,1,0:T(8,128)S(1)} %add.3.own), channel_id=1, source_target_pairs={{1,18},{2,17},{3,20},{4,19},{5,22},{6,21},{7,24},{8,23},{9,26},{10... | collective-permute-start | bytes 294920 | tf_op jit(solution)/shard_map/ppermute | solution.py:384
  210.4 1.9 collective-permute-start.22
  212.4 0.7 collective-permute-start.20
  213.2 5.2 %collective-permute-start.19 = (f32[12,16,128]{2,1,0:T(8,128)S(1)}, f32[12,16,128]{2,1,0:T(8,128)S(1)}, u32[]{:S(2)}, u32[]{:S(2)}) collective-permute-start(f32[12,16,128]{2,1,0:T(8,128)S(1)} %add.3.own), channel_id=1, source_target_pairs={{0,16},{1,17},{2,18},{3,19},{4,20},{5,21},{6,22},{7,23},{8,24},{9,... | collective-permute-start | bytes 294920 | tf_op jit(solution)/shard_map/ppermute | solution.py:384
  218.5 2.5 collective-permute-done.19.ye
  221.1 0.6 copy-done.18
  221.7 19.5 %shard_map.63 = (f32[1536,128]{1,0:T(8,128)}, f32[6,26,40,128]{3,2,1,0:T(8,128)}, f32[26,40,128]{2,1,0:T(8,128)}) custom-call(f32[12,16,128]{2,1,0:T(8,128)} %copy-done.6, f32[12,16,128]{2,1,0:T(8,128)} %copy-done.18, f32[12,16,128]{2,1,0:T(8,128)} %copy-done.17, f32[12,16,128]{2,1,0:T(8,128)} %copy-done.16, f32[12,16,128]{2,1,0:T(8,128)} %copy-done.15, ...), custom_call_target="tpu_custom_call" | custom-call | tf_op jit(solution)/shard_map/pallas_call | solution.py:399
  241.3 24.7 %all_to_all.10 = f32[64,24,128]{2,1,0:T(8,128)} all-to-all(f32[64,24,128]{2,1,0:T(8,128)} %bitcast.7), channel_id=1, replica_groups=mesh['gx'=2,'gy'=4,'gz_0'=4,'gz_1'=4] {'gy','gz_0','gz_1'}, dimensions={0} | all-to-all | bytes 1572864 | tf_op jit(solution)/shard_map/all_to_all | solution.py:876
  265.9 84.0 %shard_map.64 = (f32[48,48,48]{2,1,0:T(8,128)}, f32[48,48,48]{2,1,0:T(8,128)}, f32[8,128]{1,0:T(8,128)}) custom-call(f32[1536,128]{1,0:T(8,128)} %bitcast.6, f32[6,26,40,128]{3,2,1,0:T(8,128)} %get-tuple-element.52.stack_2_in, f32[26,40,128]{2,1,0:T(8,128)} %get-tuple-element.53.iterate_2_in, f32[6,34,40,128]{3,2,1,0:T(8,128)} %get-tuple-element.54.stack_1_in, ...), custom_call_target="tpu_custom_call" | custom-call | tf_op jit(solution)/shard_map/pallas_call | solution.py:399
  350.0 0.7 slice_bitcast_fusion
  350.7 13.6 %all_to_all.11 = f32[128,1,128]{2,1,0:T(1,128)S(1)} all-to-all(f32[128,1,128]{2,1,0:T(1,128)S(1)} %broadcast_in_dim.8), channel_id=1, replica_groups=mesh['gx'=2,'gy'=4,'gz_0'=4,'gz_1'=4] {'gx','gy','gz_0','gz_1'}, dimensions={0} | all-to-all | bytes 131072 | tf_op jit(solution)/shard_map/all_to_all | solution.py:895
  364.3 0.6 fusion
  (74 shorter events, 1.1 us)
Async XLA Ops:
  31.6 2.9 collective-permute-start
  34.4 0.9 copy-start
  44.5 28.2 %collective-permute-start.3 = (f32[19,48,128]{2,1,0:T(8,128)}, f32[19,48,128]{2,1,0:T(8,128)S(1)}, u32[]{:S(2)}, u32[]{:S(2)}) collective-permute-start(f32[19,48,128]{2,1,0:T(8,128)} %get-tuple-element.34), channel_id=1, source_target_pairs={{0,1},{1,0},{2,3},{3,2},{4,5},{5,4},{6,7},{7,6},{8,9},{9,8},{10,11... | collective-permute-start | bytes 1400840 | tf_op jit(solution)/shard_map/ppermute | solution.py:384
  44.8 27.9 %collective-permute-start.4 = (f32[19,48,128]{2,1,0:T(8,128)}, f32[19,48,128]{2,1,0:T(8,128)S(1)}, u32[]{:S(2)}, u32[]{:S(2)}) collective-permute-start(f32[19,48,128]{2,1,0:T(8,128)} %get-tuple-element.35), channel_id=1, source_target_pairs={{1,2},{2,1},{3,4},{4,3},{5,6},{6,5},{7,8},{8,7},{9,10},{10,9},{11,... | collective-permute-start | bytes 1400840 | tf_op jit(solution)/shard_map/ppermute | solution.py:384
  49.3 23.3 %collective-permute-start.1 = (f32[56,16,128]{2,1,0:T(8,128)}, f32[56,16,128]{2,1,0:T(8,128)S(1)}, u32[]{:S(2)}, u32[]{:S(2)}) collective-permute-start(f32[56,16,128]{2,1,0:T(8,128)} %get-tuple-element.32), channel_id=1, source_target_pairs={{0,16},{1,17},{2,18},{3,19},{4,20},{5,21},{6,22},{7,23},{8,24},{9,... | collective-permute-start | bytes 1376264 | tf_op jit(solution)/shard_map/ppermute | solution.py:384
  50.9 21.8 %collective-permute-start.2 = (f32[56,16,128]{2,1,0:T(8,128)}, f32[56,16,128]{2,1,0:T(8,128)S(1)}, u32[]{:S(2)}, u32[]{:S(2)}) collective-permute-start(f32[56,16,128]{2,1,0:T(8,128)} %get-tuple-element.33), channel_id=1, source_target_pairs={{16,32},{17,33},{18,34},{19,35},{20,36},{21,37},{22,38},{23,39},{2... | collective-permute-start | bytes 1376264 | tf_op jit(solution)/shard_map/ppermute | solution.py:384
  51.5 10.7 %collective-permute-start.5 = (f32[19,8,128]{2,1,0:T(8,128)}, f32[19,8,128]{2,1,0:T(8,128)S(1)}, u32[]{:S(2)}, u32[]{:S(2)}) collective-permute-start(f32[19,8,128]{2,1,0:T(8,128)} %get-tuple-element.36), channel_id=1, source_target_pairs={{0,17},{1,16},{2,19},{3,18},{4,21},{5,20},{6,23},{7,22},{8,25},{9,... | collective-permute-start | bytes 233480 | tf_op jit(solution)/shard_map/ppermute | solution.py:384
  62.2 10.5 %copy-start.19 = (f32[19,8,128]{2,1,0:T(8,128)}, f32[19,8,128]{2,1,0:T(8,128)S(1)}, u32[]{:S(2)}) copy-start(f32[19,8,128]{2,1,0:T(8,128)S(1)} %collective-permute-done.5.ee) | copy-start | bytes 233476
  62.2 9.0 %collective-permute-start.6 = (f32[19,8,128]{2,1,0:T(8,128)}, f32[19,8,128]{2,1,0:T(8,128)S(1)}, u32[]{:S(2)}, u32[]{:S(2)}) collective-permute-start(f32[19,8,128]{2,1,0:T(8,128)} %get-tuple-element.37), channel_id=1, source_target_pairs={{1,18},{2,17},{3,20},{4,19},{5,22},{6,21},{7,24},{8,23},{9,26},{10... | collective-permute-start | bytes 233480 | tf_op jit(solution)/shard_map/ppermute | solution.py:384
  71.2 1.5 copy-start.20
  71.2 0.7 collective-permute-start.7
  71.9 0.8 copy-start.21
  71.9 0.7 collective-permute-start.8
  72.6 0.8 copy-start.4
  72.7 0.9 copy-start.5
  72.7 1.1 copy-start.2
  73.7 0.8 copy-start.3
  117.7 2.2 collective-permute-start.9
  119.8 0.8 copy-start.1
  124.7 27.4 %collective-permute-start.14 = (f32[11,8,128]{2,1,0:T(8,128)}, f32[11,8,128]{2,1,0:T(8,128)S(1)}, u32[]{:S(2)}, u32[]{:S(2)}) collective-permute-start(f32[11,8,128]{2,1,0:T(8,128)} %get-tuple-element.46), channel_id=1, source_target_pairs={{0,17},{1,16},{2,19},{3,18},{4,21},{5,20},{6,23},{7,22},{8,25},{9,... | collective-permute-start | bytes 135176 | tf_op jit(solution)/shard_map/ppermute | solution.py:384
  132.1 20.7 %collective-permute-start.15 = (f32[11,8,128]{2,1,0:T(8,128)}, f32[11,8,128]{2,1,0:T(8,128)S(1)}, u32[]{:S(2)}, u32[]{:S(2)}) collective-permute-start(f32[11,8,128]{2,1,0:T(8,128)} %get-tuple-element.47), channel_id=1, source_target_pairs={{1,18},{2,17},{3,20},{4,19},{5,22},{6,21},{7,24},{8,23},{9,26},{10... | collective-permute-start | bytes 135176 | tf_op jit(solution)/shard_map/ppermute | solution.py:384
  143.0 14.3 %collective-permute-start.12 = (f32[11,24,128]{2,1,0:T(8,128)}, f32[11,24,128]{2,1,0:T(8,128)S(1)}, u32[]{:S(2)}, u32[]{:S(2)}) collective-permute-start(f32[11,24,128]{2,1,0:T(8,128)} %get-tuple-element.44), channel_id=1, source_target_pairs={{0,1},{1,0},{2,3},{3,2},{4,5},{5,4},{6,7},{7,6},{8,9},{9,8},{10,11... | collective-permute-start | bytes 405512 | tf_op jit(solution)/shard_map/ppermute | solution.py:384
  143.1 14.3 %collective-permute-start.13 = (f32[11,24,128]{2,1,0:T(8,128)}, f32[11,24,128]{2,1,0:T(8,128)S(1)}, u32[]{:S(2)}, u32[]{:S(2)}) collective-permute-start(f32[11,24,128]{2,1,0:T(8,128)} %get-tuple-element.45), channel_id=1, source_target_pairs={{1,2},{2,1},{3,4},{4,3},{5,6},{6,5},{7,8},{8,7},{9,10},{10,9},{11,... | collective-permute-start | bytes 405512 | tf_op jit(solution)/shard_map/ppermute | solution.py:384
  152.0 5.3 %collective-permute-start.10 = (f32[32,8,128]{2,1,0:T(8,128)}, f32[32,8,128]{2,1,0:T(8,128)S(1)}, u32[]{:S(2)}, u32[]{:S(2)}) collective-permute-start(f32[32,8,128]{2,1,0:T(8,128)} %get-tuple-element.42), channel_id=1, source_target_pairs={{0,16},{1,17},{2,18},{3,19},{4,20},{5,21},{6,22},{7,23},{8,24},{9,... | collective-permute-start | bytes 393224 | tf_op jit(solution)/shard_map/ppermute | solution.py:384
  152.1 5.2 %copy-start.23 = (f32[11,8,128]{2,1,0:T(8,128)}, f32[11,8,128]{2,1,0:T(8,128)S(1)}, u32[]{:S(2)}) copy-start(f32[11,8,128]{2,1,0:T(8,128)S(1)} %collective-permute-done.14.ee) | copy-start | bytes 135172
  152.1 5.2 %collective-permute-start.11 = (f32[32,8,128]{2,1,0:T(8,128)}, f32[32,8,128]{2,1,0:T(8,128)S(1)}, u32[]{:S(2)}, u32[]{:S(2)}) collective-permute-start(f32[32,8,128]{2,1,0:T(8,128)} %get-tuple-element.43), channel_id=1, source_target_pairs={{16,32},{17,33},{18,34},{19,35},{20,36},{21,37},{22,38},{23,39},{2... | collective-permute-start | bytes 393224 | tf_op jit(solution)/shard_map/ppermute | solution.py:384
  152.8 4.5 %copy-start.24 = (f32[11,8,128]{2,1,0:T(8,128)}, f32[11,8,128]{2,1,0:T(8,128)S(1)}, u32[]{:S(2)}) copy-start(f32[11,8,128]{2,1,0:T(8,128)S(1)} %collective-permute-done.15.eo) | copy-start | bytes 135172
  152.8 0.7 collective-permute-start.16
  153.5 3.8 %copy-start.25 = (f32[11,8,128]{2,1,0:T(8,128)}, f32[11,8,128]{2,1,0:T(8,128)S(1)}, u32[]{:S(2)}) copy-start(f32[11,8,128]{2,1,0:T(8,128)S(1)} %collective-permute-done.16.oe) | copy-start | bytes 135172
  153.5 0.7 collective-permute-start.17
  154.2 3.1 copy-start.26
  181.0 1.6 collective-permute-start.18
  183.5 37.5 %copy-start.6 = (f32[12,16,128]{2,1,0:T(8,128)}, f32[12,16,128]{2,1,0:T(8,128)S(1)}, u32[]{:S(2)}) copy-start(f32[12,16,128]{2,1,0:T(8,128)S(1)} %add.3.own) | copy-start | bytes 294916
  183.5 28.8 %collective-permute-start.26 = (f32[12,16,128]{2,1,0:T(8,128)S(1)}, f32[12,16,128]{2,1,0:T(8,128)S(1)}, u32[]{:S(2)}, u32[]{:S(2)}) collective-permute-start(f32[12,16,128]{2,1,0:T(8,128)S(1)} %add.3.own), channel_id=1, source_target_pairs={{17,34},{18,33},{19,36},{20,35},{21,38},{22,37},{23,40},{24,39},{2... | collective-permute-start | bytes 294920 | tf_op jit(solution)/shard_map/ppermute | solution.py:384
  184.2 28.2 %collective-permute-start.25 = (f32[12,16,128]{2,1,0:T(8,128)S(1)}, f32[12,16,128]{2,1,0:T(8,128)S(1)}, u32[]{:S(2)}, u32[]{:S(2)}) collective-permute-start(f32[12,16,128]{2,1,0:T(8,128)S(1)} %add.3.own), channel_id=1, source_target_pairs={{16,33},{17,32},{18,35},{19,34},{20,37},{21,36},{22,39},{23,38},{2... | collective-permute-start | bytes 294920 | tf_op jit(solution)/shard_map/ppermute | solution.py:384
  184.9 28.3 %collective-permute-start.24 = (f32[12,16,128]{2,1,0:T(8,128)S(1)}, f32[12,16,128]{2,1,0:T(8,128)S(1)}, u32[]{:S(2)}, u32[]{:S(2)}) collective-permute-start(f32[12,16,128]{2,1,0:T(8,128)S(1)} %add.3.own), channel_id=1, source_target_pairs={{1,18},{2,17},{3,20},{4,19},{5,22},{6,21},{7,24},{8,23},{9,26},{10... | collective-permute-start | bytes 294920 | tf_op jit(solution)/shard_map/ppermute | solution.py:384
  210.3 8.2 %collective-permute-start.23 = (f32[12,16,128]{2,1,0:T(8,128)S(1)}, f32[12,16,128]{2,1,0:T(8,128)S(1)}, u32[]{:S(2)}, u32[]{:S(2)}) collective-permute-start(f32[12,16,128]{2,1,0:T(8,128)S(1)} %add.3.own), channel_id=1, source_target_pairs={{0,17},{1,16},{2,19},{3,18},{4,21},{5,20},{6,23},{7,22},{8,25},{9,... | collective-permute-start | bytes 294920 | tf_op jit(solution)/shard_map/ppermute | solution.py:384
  210.4 8.1 %collective-permute-start.22 = (f32[12,16,128]{2,1,0:T(8,128)S(1)}, f32[12,16,128]{2,1,0:T(8,128)S(1)}, u32[]{:S(2)}, u32[]{:S(2)}) collective-permute-start(f32[12,16,128]{2,1,0:T(8,128)S(1)} %add.3.own), channel_id=1, source_target_pairs={{1,2},{2,1},{3,4},{4,3},{5,6},{6,5},{7,8},{8,7},{9,10},{10,9},{11,... | collective-permute-start | bytes 294920 | tf_op jit(solution)/shard_map/ppermute | solution.py:384
  212.3 8.7 %copy-start.11 = (f32[12,16,128]{2,1,0:T(8,128)}, f32[12,16,128]{2,1,0:T(8,128)S(1)}, u32[]{:S(2)}) copy-start(f32[12,16,128]{2,1,0:T(8,128)S(1)} %collective-permute-done.26.oo) | copy-start | bytes 294916
  212.3 6.1 %collective-permute-start.21 = (f32[12,16,128]{2,1,0:T(8,128)S(1)}, f32[12,16,128]{2,1,0:T(8,128)S(1)}, u32[]{:S(2)}, u32[]{:S(2)}) collective-permute-start(f32[12,16,128]{2,1,0:T(8,128)S(1)} %add.3.own), channel_id=1, source_target_pairs={{0,1},{1,0},{2,3},{3,2},{4,5},{5,4},{6,7},{7,6},{8,9},{9,8},{10,11... | collective-permute-start | bytes 294920 | tf_op jit(solution)/shard_map/ppermute | solution.py:384
  212.4 8.6 %copy-start.12 = (f32[12,16,128]{2,1,0:T(8,128)}, f32[12,16,128]{2,1,0:T(8,128)S(1)}, u32[]{:S(2)}) copy-start(f32[12,16,128]{2,1,0:T(8,128)S(1)} %collective-permute-done.25.oe) | copy-start | bytes 294916
  212.4 6.1 %collective-permute-start.20 = (f32[12,16,128]{2,1,0:T(8,128)S(1)}, f32[12,16,128]{2,1,0:T(8,128)S(1)}, u32[]{:S(2)}, u32[]{:S(2)}) collective-permute-start(f32[12,16,128]{2,1,0:T(8,128)S(1)} %add.3.own), channel_id=1, source_target_pairs={{16,32},{17,33},{18,34},{19,35},{20,36},{21,37},{22,38},{23,39},{2... | collective-permute-start | bytes 294920 | tf_op jit(solution)/shard_map/ppermute | solution.py:384
  213.2 7.8 %copy-start.13 = (f32[12,16,128]{2,1,0:T(8,128)}, f32[12,16,128]{2,1,0:T(8,128)S(1)}, u32[]{:S(2)}) copy-start(f32[12,16,128]{2,1,0:T(8,128)S(1)} %collective-permute-done.24.eo) | copy-start | bytes 294916
  213.2 7.8 %collective-permute-start.19 = (f32[12,16,128]{2,1,0:T(8,128)S(1)}, f32[12,16,128]{2,1,0:T(8,128)S(1)}, u32[]{:S(2)}, u32[]{:S(2)}) collective-permute-start(f32[12,16,128]{2,1,0:T(8,128)S(1)} %add.3.own), channel_id=1, source_target_pairs={{0,16},{1,17},{2,18},{3,19},{4,20},{5,21},{6,22},{7,23},{8,24},{9,... | collective-permute-start | bytes 294920 | tf_op jit(solution)/shard_map/ppermute | solution.py:384
  218.4 2.6 copy-start.14
  218.4 2.6 copy-start.15
  218.5 2.6 copy-start.16
  218.5 2.6 copy-start.17
  (6 other events, 4.0 us)
